TPU v7x, 32 devices: a whole 2x2x4 slice. The times are simulated.
32 devices in a mesh: tm: 4 (over x, core), space: 8 (over z, y).
Axes of the slice: x: 2, y: 2, z: 4, core: 2. Of those that a mesh axis runs over, the one named last changes fastest.
Arguments:
- start_value: float32 [4, 8, 512, 256], P('tm', 'space'), may hold values from -6 to 6
- old_nodes: float32 [4, 3, 8, 512, 256], P('tm', None, 'space'), may hold values from -6 to 6
- diffusivity: float32 [8, 512, 256], P('space'), may hold values from 0.2 to 2
Outputs:
- fine_nodes: float32 [4, 3, 8, 512, 256], P('tm', None, 'space')
- next_start: float32 [4, 8, 512, 256], P('tm', 'space')
- next_coarse: float32 [4, 8, 512, 256], P('tm', 'space')
All inputs are finite; a program needn't handle non-finite values.
Results may differ from a plain program's by a relative error of at most 0.0001.
Values sent between devices are 32-bit elements; how exact they have to be, the bound alone decides.
A program may use at most 64 MiB of HBM per device.

v0:
```python
import math

import jax
import jax.numpy as jnp
from jax import lax
from jax.experimental import pallas as pl
from jax.experimental.pallas import tpu as pltpu
from jax.sharding import PartitionSpec as P

STEP = 2.0
ROOT_SIX = math.sqrt(6.0)
NODE_TIMES = [(4.0 - ROOT_SIX) / 10.0, (4.0 + ROOT_SIX) / 10.0, 1.0]
COLLOC = [
    [
        (88.0 - 7.0 * ROOT_SIX) / 360.0,
        (296.0 - 169.0 * ROOT_SIX) / 1800.0,
        (-2.0 + 3.0 * ROOT_SIX) / 225.0,
    ],
    [
        (296.0 + 169.0 * ROOT_SIX) / 1800.0,
        (88.0 + 7.0 * ROOT_SIX) / 360.0,
        (-2.0 - 3.0 * ROOT_SIX) / 225.0,
    ],
    [(16.0 - ROOT_SIX) / 36.0, (16.0 + ROOT_SIX) / 36.0, 1.0 / 9.0],
]
MESH = pl.DeviceIdType.MESH
PAD = 8

KAPPA, NODE, START, RES, IMG, GAIN = 0, 1, 4, 5, 9, 13
FIELDS = 15
H_KAPPA, H_NODE, H_RES, H_IMG, H_GAIN = 0, 1, 4, 8, 12
HALOS = 14


def sweep_weight(row, column):
    below = COLLOC[row - 1][column] if row > 0 else 0.0
    return COLLOC[row][column] - below


def node_width(row):
    below = NODE_TIMES[row - 1] if row > 0 else 0.0
    return NODE_TIMES[row] - below


WIDTHS = [STEP * node_width(0), STEP * node_width(1), STEP * node_width(2), STEP]


def chunk_bounds(rows, tile):
    tiles = rows // tile
    parts = min(5, tiles)
    cuts = [tile * (-(-tiles * c // parts)) for c in range(parts + 1)]
    return [(cuts[c], cuts[c + 1] - cuts[c]) for c in range(parts)]


def tile_of(rows, most):
    best = 8
    for size in range(8, most + 1, 8):
        if rows % size == 0:
            best = size
    return best


def kernel(
    slices, slabs, ny, nz,
    start_in, nodes_in, kappa_in,
    fine_out, start_out, coarse_out,
    field, lower, upper, faces, across, result, staged, mail, sums,
    swap_s, swap_r, own_s, halo_s, halo_r, sum_s, sum_r, out_s, out_r, keep_s, end_s, end_r, copy_s,
):
    f32 = jnp.float32
    t = lax.axis_index("tm")
    s = lax.axis_index("space")
    h = lax.rem(s, 2)
    p = lax.div(s, 2)
    pairs = slabs // 2
    half = ny // 2
    win = half + PAD
    other = 1 - h
    partner = s + 1 - 2 * h
    first_row = pl.multiple_of(h * (half - PAD), 8)
    partner_row = pl.multiple_of(other * (half - PAD), 8)
    own = pl.multiple_of(PAD * h, 8)
    mine = pl.multiple_of(h * half, 8)
    has_next = t < slices - 1
    has_prev = t > 0
    has_lower = p > 0
    has_upper = p < pairs - 1
    pending = []

    def start(copy, cond=None):
        if cond is None:
            copy.start()
        else:
            pl.when(cond)(copy.start)
        return copy

    def later(copy, cond=None):
        pending.append((copy, cond))

    def remote(src, dst, send, recv, tm, space):
        return pltpu.make_async_remote_copy(
            src_ref=src, dst_ref=dst, send_sem=send, recv_sem=recv,
            device_id=(tm, space), device_id_type=MESH,
        )

    barrier = pltpu.get_barrier_semaphore()

    def greet(d, carry):
        pl.semaphore_signal(
            barrier, inc=1, device_id=(t, lax.rem(s + d, slabs)), device_id_type=MESH
        )
        return carry

    lax.fori_loop(1, slabs, greet, 0)
    for cond, tm in ((has_next, t + 1), (has_prev, t - 1)):

        @pl.when(cond)
        def _(tm=tm):
            for space in (s, partner):
                pl.semaphore_signal(barrier, inc=1, device_id=(tm, space), device_id_type=MESH)

    sources = [kappa_in.at[0]] + [nodes_in.at[0, j, 0] for j in range(3)] + [start_in.at[0, 0]]
    loads = []
    for k, source in enumerate(sources):
        loads.append(
            start(
                pltpu.make_async_copy(
                    source.at[pl.ds(first_row, win)], field.at[k, h, pl.ds(PAD, win)], own_s.at[k]
                )
            )
        )

    zeros = jnp.zeros((PAD, nz), f32)
    for k in range(FIELDS):
        for slab in range(2):
            field[k, slab, 0:PAD, :] = zeros
            field[k, slab, win + PAD : win + 2 * PAD, :] = zeros

    def clear(ref):
        def body(i, carry):
            for k in range(HALOS):
                ref[k, pl.ds(pl.multiple_of(i * 8, 8), 8), :] = zeros
            return carry

        lax.fori_loop(0, win // 8, body, 0)

    @pl.when(jnp.logical_not(has_lower))
    def _():
        clear(lower)

    @pl.when(jnp.logical_not(has_upper))
    def _():
        clear(upper)

    pl.semaphore_wait(
        barrier,
        slabs - 1 + 2 * has_next.astype(jnp.int32) + 2 * has_prev.astype(jnp.int32),
    )

    tile = tile_of(win, 24)
    bounds = chunk_bounds(win, tile)
    chunks = len(bounds)

    def swap_copy(k, c):
        lo, rows = bounds[c]
        return remote(
            sources[k].at[pl.ds(partner_row + lo, rows)],
            field.at[k, h, pl.ds(PAD + lo, rows)],
            swap_s.at[k, c], swap_r.at[k, c], t, partner,
        )

    def swap_wait(k, c):
        lo, rows = bounds[c]
        dst = field.at[k, other, pl.ds(PAD + lo, rows)]
        remote(dst, dst, swap_s.at[k, c], swap_r.at[k, c], t, partner).wait_recv()

    for c in range(chunks):
        for k in range(5):
            later(start(swap_copy(k, c)))

    def down(f, k, c, lo, rows):
        return remote(
            field.at[f, 0, pl.ds(PAD + lo, rows)], upper.at[k, pl.ds(lo, rows)],
            halo_s.at[k, 0, c], halo_r.at[k, 0, c], t, s - 2,
        )

    def up(f, k, c, lo, rows):
        return remote(
            field.at[f, 1, pl.ds(PAD + lo, rows)], lower.at[k, pl.ds(lo, rows)],
            halo_s.at[k, 1, c], halo_r.at[k, 1, c], t, s + 2,
        )

    def first_hop(k, c, which):
        @pl.when(jnp.logical_and(which == 0, has_lower))
        def _():
            down(k, k, c, *bounds[c]).start()

        @pl.when(jnp.logical_and(which == 1, has_upper))
        def _():
            up(k, k, c, *bounds[c]).start()

    for copy in loads:
        copy.wait()
    for c in range(chunks):
        for k in range(4):
            first_hop(k, c, h)

    def halo_wait(k, c, lo, rows, sides=(0, 1)):
        if 0 in sides:

            @pl.when(has_upper)
            def _():
                remote(
                    upper.at[k, pl.ds(lo, rows)], upper.at[k, pl.ds(lo, rows)],
                    halo_s.at[k, 0, c], halo_r.at[k, 0, c], t, s + 2,
                ).wait_recv()

        if 1 in sides:

            @pl.when(has_lower)
            def _():
                remote(
                    lower.at[k, pl.ds(lo, rows)], lower.at[k, pl.ds(lo, rows)],
                    halo_s.at[k, 1, c], halo_r.at[k, 1, c], t, s - 2,
                ).wait_recv()

    def halo_sent(f, k, c, lo, rows):
        later(down(f, k, c, lo, rows), has_lower)
        later(up(f, k, c, lo, rows), has_upper)

    for k in range(4):
        for c in range(chunks):
            halo_sent(k, k, c, *bounds[c])

    lane = lax.broadcasted_iota(jnp.int32, (tile, nz), 1)

    def loop(rows, size, body, init=0, offset=0):
        def step(i, carry):
            return body(pl.multiple_of(offset + i * size, 8), carry)

        return lax.fori_loop(0, rows // size, step, init)

    def coefficients(b, carry):
        windows = [field[KAPPA, slab, pl.ds(b, tile + 2 * PAD), :] for slab in range(2)]
        centre = [w[PAD : PAD + tile] for w in windows]
        before = 0.5 * (centre[0] + lower[H_KAPPA, pl.ds(b, tile), :])
        between = 0.5 * (centre[0] + centre[1])
        after = 0.5 * (centre[1] + upper[H_KAPPA, pl.ds(b, tile), :])
        across[0, pl.ds(b, tile), :] = before
        across[1, pl.ds(b, tile), :] = between
        across[2, pl.ds(b, tile), :] = after
        ends = [before + between, between + after]
        for slab in range(2):
            w, k = windows[slab], centre[slab]
            above = 0.5 * (k + w[PAD - 1 : PAD - 1 + tile])
            below = 0.5 * (k + w[PAD + 1 : PAD + 1 + tile])
            right = jnp.where(lane == nz - 1, 0.0, pltpu.roll(k, nz - 1, axis=1))
            left = jnp.where(lane == 0, 0.0, pltpu.roll(k, 1, axis=1))
            right_face = 0.5 * (k + right)
            left_face = 0.5 * (k + left)
            faces[0, slab, pl.ds(b, tile), :] = above
            faces[1, slab, pl.ds(b, tile), :] = below
            faces[2, slab, pl.ds(b, tile), :] = jnp.where(lane == nz - 1, 0.0, right_face)
            faces[3, slab, pl.ds(b, tile), :] = ends[slab] + above + below + right_face + left_face
        return carry

    def heat(windows, outer, b, size):
        centre = [w[PAD : PAD + size] for w in windows]
        between = across[1, pl.ds(b, size), :]
        images = []
        for slab in range(2):
            w, v = windows[slab], centre[slab]
            fz = faces[2, slab, pl.ds(b, size), :]
            value = between * centre[1 - slab]
            if outer[slab] is not None:
                value = value + outer[slab]
            value = value + faces[0, slab, pl.ds(b, size), :] * w[PAD - 1 : PAD - 1 + size]
            value = value + faces[1, slab, pl.ds(b, size), :] * w[PAD + 1 : PAD + 1 + size]
            value = value + fz * pltpu.roll(v, nz - 1, axis=1) + pltpu.roll(fz * v, 1, axis=1)
            images.append(value - faces[3, slab, pl.ds(b, size), :] * v)
        return centre, images

    def plain_heat(f, k, b, size):
        windows = [field[f, slab, pl.ds(b, size + 2 * PAD), :] for slab in range(2)]
        outer = (
            across[0, pl.ds(b, size), :] * lower[k, pl.ds(b, size), :],
            across[2, pl.ds(b, size), :] * upper[k, pl.ds(b, size), :],
        )
        return heat(windows, outer, b, size)

    def folded(value):
        return jnp.sum(value.reshape(-1, 8, nz), axis=0)

    def sum_copy(e, d):
        return remote(
            sums.at[e, s], sums.at[e, s], sum_s.at[e, d], sum_r.at[e, d],
            t, lax.rem(s + d, slabs),
        )

    def sum_start(e, parts):
        for row, part in enumerate(parts):
            flat = jnp.sum(part, axis=0, keepdims=True)
            line = flat[:, 0:128]
            for at in range(128, nz, 128):
                line = line + flat[:, at : at + 128]
            sums[e, s, row : row + 1, :] = line

        def body(d, carry):
            sum_copy(e, d).start()
            return carry

        lax.fori_loop(1, slabs, body, 0)

    def sum_wait(e):
        def body(d, carry):
            source = lax.rem(s - d + slabs, slabs)
            remote(
                sums.at[e, source], sums.at[e, source], sum_s.at[e, d], sum_r.at[e, d],
                t, source,
            ).wait_recv()
            return carry

        lax.fori_loop(1, slabs, body, 0)
        total = jnp.sum(sums[e], axis=0)
        total = jnp.sum(total, axis=1, keepdims=True)
        return total[0:1, :], total[1:2, :]

    def halo_send(f, k, c, lo, rows):
        start(down(f, k, c, lo, rows), has_lower)
        start(up(f, k, c, lo, rows), has_upper)
        halo_sent(f, k, c, lo, rows)

    quarter = half // 2
    set_up = own
    set_down = pl.multiple_of(own + quarter, 8)
    pieces_of = (
        ((quarter, quarter + PAD), (0, quarter + PAD)),
        ((0, quarter), (quarter + PAD, quarter)),
    )

    def img_send(m, piece):
        (lo_d, rows_d), (lo_u, rows_u) = pieces_of[piece]
        copies = (
            (down(IMG + m, H_IMG + m, piece, lo_d, rows_d), has_lower),
            (up(IMG + m, H_IMG + m, piece, lo_u, rows_u), has_upper),
        )
        for copy, cond in copies:
            start(copy, cond)
            later(copy, cond)

    def img_wait(m, piece):
        halo_wait(H_IMG + m, piece, *pieces_of[piece][0], (0,))
        halo_wait(H_IMG + m, piece, *pieces_of[piece][1], (1,))

    def product(m):
        def body(b, carry):
            centre, images = plain_heat(RES + m, H_RES + m, b, tile)
            row = lax.broadcasted_iota(jnp.int32, (tile, nz), 0) + b
            inside = jnp.logical_and(row >= own, row < own + half)
            norm, along = carry
            for slab in range(2):
                v = centre[slab]
                z = v - WIDTHS[m] * images[slab]
                field[IMG + m, slab, pl.ds(PAD + b, tile), :] = z
                masked = jnp.where(inside, v, 0.0)
                norm = norm + folded(masked * v)
                along = along + folded(masked * z)
            return norm, along

        nothing = jnp.zeros((8, nz), f32)
        norm, along = loop(win, tile, body, (nothing, nothing))
        sum_start(2 * m, (norm, along))
        img_send(m, 0)

    small = tile_of(quarter, 32)

    def second(m):
        norm_now, along = sum_wait(2 * m)
        step_size = norm_now / along
        img_wait(m, 0)

        def body_of(side):
            ref = lower if side == 0 else upper

            def body(b, carry):
                windows = [
                    field[RES + m, slab, pl.ds(b, small + 2 * PAD), :]
                    - step_size * field[IMG + m, slab, pl.ds(b, small + 2 * PAD), :]
                    for slab in range(2)
                ]
                beside = (
                    ref[H_RES + m, pl.ds(b, small), :]
                    - step_size * ref[H_IMG + m, pl.ds(b, small), :]
                )
                term = 2.0 * across[2 * side, pl.ds(b, small), :] * beside
                outer = (term, None) if side == 0 else (None, term)
                centre, images = heat(windows, outer, b, small)
                norm, along = carry
                for slab in range(2):
                    v = centre[slab]
                    norm = norm + folded(v * v)
                    along = along + folded(v * (v - WIDTHS[m] * images[slab]))
                return norm, along

            return body

        nothing = jnp.zeros((8, nz), f32)
        carry = loop(quarter, small, body_of(0), (nothing, nothing), set_up)
        carry = loop(quarter, small, body_of(1), carry, set_down)
        sum_start(2 * m + 1, carry)
        return norm_now, step_size

    def factors(m, norm_now, step_size):
        norm_next, along = sum_wait(2 * m + 1)
        momentum = norm_next / norm_now
        step_next = norm_next / (along - momentum * norm_next / step_size)
        return step_size + step_next * (1.0 + momentum), step_size * step_next

    def advance(m, scalars):
        on_res, on_img = scalars
        for c in range(chunks):
            halo_wait(H_GAIN + m, c, *spans[c])
        img_wait(m, 1)

        def body(b, carry):
            at = pl.ds(PAD + b, tile)
            rows = pl.ds(b, tile)
            for slab in range(2):
                field[RES + m + 1, slab, at, :] = (
                    field[GAIN + m, slab, at, :]
                    + on_res * field[RES + m, slab, at, :]
                    - on_img * field[IMG + m, slab, at, :]
                )
            for ref in (lower, upper):
                ref[H_RES + m + 1, rows, :] = (
                    ref[H_GAIN + m, rows, :]
                    + on_res * ref[H_RES + m, rows, :]
                    - on_img * ref[H_IMG + m, rows, :]
                )
            return carry

        loop(win, tile, body)

    def coarse_residual():
        def body(b, carry):
            at = pl.ds(PAD + b, tile)
            rows = pl.ds(b, tile)
            for slab in range(2):
                field[RES + 3, slab, at, :] = (
                    field[RES, slab, at, :] + field[GAIN, slab, at, :] + field[GAIN + 1, slab, at, :]
                )
            for ref in (lower, upper):
                ref[H_RES + 3, rows, :] = (
                    ref[H_RES, rows, :] + ref[H_GAIN, rows, :] + ref[H_GAIN + 1, rows, :]
                )
            return carry

        loop(win, tile, body)

    def finish(m, scalars):
        on_res, on_img = scalars
        node = NODE + min(m, 2)

        def body(b, carry):
            for slab in range(2):
                at = pl.ds(PAD + b, small)
                result[m, slab, pl.ds(b, small), :] = (
                    field[node, slab, at, :]
                    + on_res * field[RES + m, slab, at, :]
                    - on_img * field[IMG + m, slab, at, :]
                )
            return carry

        loop(half, small, body, 0, own)

    def residuals(b, carry):
        images = [plain_heat(NODE + j, H_NODE + j, b, tile)[1] for j in range(3)]
        at = pl.ds(PAD + b, tile)
        for slab in range(2):
            nodes = [field[NODE + j, slab, at, :] for j in range(3)]
            ahead = [field[START, slab, at, :]] + nodes
            for row, f in enumerate((RES, GAIN, GAIN + 1)):
                value = ahead[row] - nodes[row]
                for j in range(3):
                    value = value + (STEP * sweep_weight(row, j)) * images[j][slab]
                field[f, slab, at, :] = value
        return carry

    spans = []
    for c, (lo, rows) in enumerate(bounds):
        begin = lo - tile if c else 0
        end = lo + rows - (tile if c < chunks - 1 else 0)
        spans.append((begin, end - begin))

    def begin_rows(c):
        for k in range(4):
            halo_wait(k, c, *bounds[c])
        lo, rows = spans[c]
        loop(rows, tile, coefficients, 0, lo)
        loop(rows, tile, residuals, 0, lo)
        halo_send(RES, H_RES, c, lo, rows)
        if c == 0:
            halo_send(GAIN, H_GAIN, c, lo, rows)

    order = [(k, c) for c in range(chunks) for k in range(5)]
    ready = {}
    for c in range(chunks):
        ready[min(5 * c + 6, len(order) - 1)] = c
    for n, (k, c) in enumerate(order):
        swap_wait(k, c)
        if k < 4:
            first_hop(k, c, other)
        if n in ready:
            begin_rows(ready[n])
    for c in range(1, chunks - 1):
        halo_send(GAIN, H_GAIN, c, *spans[c])

    def give_back(m):
        later(
            start(
                remote(
                    result.at[m, other, pl.ds(own, half)], fine_out.at[0, m, 0, pl.ds(mine, half)],
                    out_s.at[m], out_r.at[m], t, partner,
                )
            )
        )
        keep = pltpu.make_async_copy(
            result.at[m, h, pl.ds(own, half)], fine_out.at[0, m, 0, pl.ds(mine, half)], keep_s.at[m]
        )
        keep.start()
        return keep

    theirs = pl.multiple_of(other * half, 8)

    @pl.when(jnp.logical_not(has_prev))
    def _():
        pltpu.make_async_copy(start_in.at[0, 0], staged, copy_s.at[0]).start()

    for c in range(chunks):
        halo_wait(H_RES, c, *spans[c])
    product(0)
    halo_send(GAIN, H_GAIN, chunks - 1, *spans[chunks - 1])
    scalars = second(0)
    img_send(0, 1)
    halo_send(GAIN + 1, H_GAIN + 1, 0, *spans[0])
    update = factors(0, *scalars)
    advance(0, update)
    product(1)
    for c in range(1, chunks - 1):
        halo_send(GAIN + 1, H_GAIN + 1, c, *spans[c])
    finish(0, update)
    keeps = [give_back(0)]
    @pl.when(jnp.logical_not(has_prev))
    def _():
        pltpu.make_async_copy(start_in.at[0, 0], staged, copy_s.at[0]).wait()
        first = pltpu.make_async_copy(staged, start_out.at[0, 0], copy_s.at[0])
        second_copy = pltpu.make_async_copy(staged, coarse_out.at[0, 0], copy_s.at[1])
        first.start()
        second_copy.start()
        first.wait()
        second_copy.wait()

    scalars = second(1)
    img_send(1, 1)
    halo_send(GAIN + 1, H_GAIN + 1, chunks - 1, *spans[chunks - 1])
    update = factors(1, *scalars)
    advance(1, update)
    product(2)
    coarse_residual()
    product(3)
    scalars = second(2)
    finish(1, update)
    keeps.append(give_back(1))
    scalars_coarse = second(3)
    finish(2, factors(2, *scalars))
    pieces = 2
    piece = half // pieces
    for c in range(pieces):
        later(
            start(
                remote(
                    result.at[2, other, pl.ds(own + c * piece, piece)],
                    mail.at[pl.ds(c * piece, piece)],
                    out_s.at[2 + c], out_r.at[2 + c], t, partner,
                )
            )
        )
    for c in range(pieces):
        rows = pl.ds(mine + c * piece, piece)
        src = result.at[2, h, pl.ds(own + c * piece, piece)]
        copy = remote(src, start_out.at[0, 0, rows], end_s.at[2 + c], end_r.at[2 + c], t + 1, s)
        start(copy, has_next)
        later(copy, has_next)
        keep = pltpu.make_async_copy(src, fine_out.at[0, 2, 0, rows], keep_s.at[2 + c])
        keep.start()
        keeps.append(keep)
    finish(3, factors(3, *scalars_coarse))

    def coarse_copies():
        return [
            remote(
                result.at[3, h, pl.ds(own, half)], coarse_out.at[0, 0, pl.ds(mine, half)],
                end_s.at[0], end_r.at[0], t + 1, s,
            ),
            remote(
                result.at[3, other, pl.ds(own, half)], coarse_out.at[0, 0, pl.ds(mine, half)],
                end_s.at[1], end_r.at[1], t + 1, partner,
            ),
        ]

    for copy in coarse_copies():
        start(copy, has_next)
        later(copy, has_next)

    for c in range(pieces):
        rows = pl.ds(theirs + c * piece, piece)
        src = mail.at[pl.ds(c * piece, piece)]
        remote(src, src, out_s.at[2 + c], out_r.at[2 + c], t, partner).wait_recv()
        copy = remote(
            src, start_out.at[0, 0, rows],
            end_s.at[2 + pieces + c], end_r.at[2 + pieces + c], t + 1, s,
        )
        start(copy, has_next)
        later(copy, has_next)
        keep = pltpu.make_async_copy(src, fine_out.at[0, 2, 0, rows], keep_s.at[2 + pieces + c])
        keep.start()
        keeps.append(keep)

    for m in range(2):
        dst = fine_out.at[0, m, 0, pl.ds(theirs, half)]
        remote(dst, dst, out_s.at[m], out_r.at[m], t, partner).wait_recv()

    @pl.when(has_prev)
    def _():
        for k in range(2):
            at = mine if k == 0 else theirs
            dst = coarse_out.at[0, 0, pl.ds(at, half)]
            remote(dst, dst, end_s.at[k], end_r.at[k], t - 1, s).wait_recv()
        for k in range(2):
            at = mine if k == 0 else theirs
            for c in range(pieces):
                dst = start_out.at[0, 0, pl.ds(at + c * piece, piece)]
                e = 2 + k * pieces + c
                remote(dst, dst, end_s.at[e], end_r.at[e], t - 1, s).wait_recv()

    for keep in keeps:
        keep.wait()
    for copy, cond in pending:
        if cond is None:
            copy.wait_send()
        else:
            pl.when(cond)(copy.wait_send)

    def drain(d, carry):
        for e in range(8):
            sum_copy(e, d).wait_send()
        return carry

    lax.fori_loop(1, slabs, drain, 0)


def solution(mesh):
    slices, slabs = mesh.shape["tm"], mesh.shape["space"]

    def on_device(start_value, old_nodes, diffusivity):
        ny, nz = start_value.shape[2:]
        half = ny // 2
        win = half + PAD
        chunks = len(chunk_bounds(win, tile_of(win, 24)))
        vmem = lambda *shape: pltpu.VMEM(shape, jnp.float32)
        dma = lambda *shape: pltpu.SemaphoreType.DMA(shape)

        def body(*refs):
            kernel(slices, slabs, ny, nz, *refs)

        return pl.pallas_call(
            body,
            out_shape=(
                jax.ShapeDtypeStruct(old_nodes.shape, jnp.float32),
                jax.ShapeDtypeStruct(start_value.shape, jnp.float32),
                jax.ShapeDtypeStruct(start_value.shape, jnp.float32),
            ),
            in_specs=[pl.BlockSpec(memory_space=pl.ANY)] * 3,
            out_specs=(pl.BlockSpec(memory_space=pl.ANY),) * 3,
            scratch_shapes=[
                vmem(FIELDS, 2, win + 2 * PAD, nz),
                vmem(HALOS, win, nz),
                vmem(HALOS, win, nz),
                vmem(4, 2, win, nz),
                vmem(3, win, nz),
                vmem(4, 2, win, nz),
                vmem(ny, nz),
                vmem(half, nz),
                vmem(8, slabs, 2, 128),
                dma(5, chunks), dma(5, chunks), dma(5),
                dma(HALOS, 2, chunks), dma(HALOS, 2, chunks),
                dma(8, slabs), dma(8, slabs),
                dma(4), dma(4), dma(6), dma(6), dma(6), dma(2),
            ],
            compiler_params=pltpu.CompilerParams(
                collective_id=0, has_side_effects=True, vmem_limit_bytes=60 * 1024 * 1024
            ),
            name="pfasst",
        )(start_value, old_nodes, diffusivity)

    in_specs = (
        P("tm", "space", None, None),
        P("tm", None, "space", None, None),
        P("space", None, None),
    )
    out_specs = (
        P("tm", None, "space", None, None),
        P("tm", "space", None, None),
        P("tm", "space", None, None),
    )
    return jax.shard_map(
        on_device, mesh=mesh, in_specs=in_specs, out_specs=out_specs, check_vma=False
    )
```

profile of v0, /device:TPU:3, one launch (start us, length us, event | category | flops | bytes accessed | tf_op | source)
XLA Modules:
  0.0 101.6 jit_solution(17917298351670181200)
XLA Ops:
  0.6 96.6 %pfasst.1 = (f32[1,3,1,512,256]{4,3,2,1,0:T(8,128)}, f32[1,1,512,256]{3,2,1,0:T(8,128)}, f32[1,1,512,256]{3,2,1,0:T(8,128)}) custom-call(f32[1,1,512,256]{3,2,1,0:T(8,128)} %refs_0_.1, f32[1,3,1,512,256]{4,3,2,1,0:T(8,128)} %refs_1_.1, f32[1,512,256]{2,1,0:T(8,128)} %refs_2_.1), custom_call_target="tpu_custom_call" | custom-call | tf_op jit(solution)/shard_map/pfasst/pallas_call | solution.py:676
  97.2 0.0 copy-start.1
  97.3 0.0 copy-start
  97.3 2.7 %copy.9 = f32[1,3,1,512,256]{4,3,2,1,0:T(8,128)} copy(f32[1,3,1,512,256]{4,3,2,1,0:T(8,128)} %get-tuple-element.6) | data formatting | bytes 3145728
  100.0 0.0 copy-done.1
  100.0 0.8 copy.10
  100.8 0.0 copy-done
  100.8 0.8 copy.11
Async XLA Ops:
  97.2 2.8 %copy-start.1 = (f32[1,1,512,256]{3,2,1,0:T(8,128)S(1)}, f32[1,1,512,256]{3,2,1,0:T(8,128)}, u32[]{:S(2)}) copy-start(f32[1,1,512,256]{3,2,1,0:T(8,128)} %get-tuple-element.7) | copy-start | bytes 1572868
  97.3 3.5 %copy-start = (f32[1,1,512,256]{3,2,1,0:T(8,128)S(1)}, f32[1,1,512,256]{3,2,1,0:T(8,128)}, u32[]{:S(2)}) copy-start(f32[1,1,512,256]{3,2,1,0:T(8,128)} %get-tuple-element.8) | copy-start | bytes 1572868
where the time goes:
time: 102 us
  Pallas kernels  96.6 us (95%)
  local copies, waits for them, and re-layouts  4.33 us (4%)
    pallas_call x1, Pallas kernels, on_device(): pl.pallas_call(body, out_shape=(jax.ShapeDtypeStruct(old_nodes.shape, jnp...  96.6 us
    unnamed x7, local copies, waits for them, and re-layouts  4.33 us

commit v1 on v0

--- a/solution.py
+++ b/solution.py
@@ -48,7 +48,11 @@
 def chunk_bounds(rows, tile):
     tiles = rows // tile
     parts = min(5, tiles)
-    cuts = [tile * (-(-tiles * c // parts)) for c in range(parts + 1)]
+    counts = [tiles // parts + (c < tiles % parts) for c in range(parts)]
+    if counts[-1] > 1:
+        counts[-1] -= 1
+        counts[1 if parts > 2 else 0] += 1
+    cuts = [tile * sum(counts[:c]) for c in range(parts + 1)]
     return [(cuts[c], cuts[c + 1] - cuts[c]) for c in range(parts)]
 
 
@@ -64,8 +68,8 @@
     slices, slabs, ny, nz,
     start_in, nodes_in, kappa_in,
     fine_out, start_out, coarse_out,
-    field, lower, upper, faces, across, result, staged, mail, sums,
-    swap_s, swap_r, own_s, halo_s, halo_r, sum_s, sum_r, out_s, out_r, keep_s, end_s, end_r, copy_s,
+    field, lower, upper, faces, across, result, sums,
+    swap_s, swap_r, own_s, halo_s, halo_r, sum_s, sum_r, out_s, out_r, end_s, end_r, copy_s,
 ):
     f32 = jnp.float32
     t = lax.axis_index("tm")
@@ -175,8 +179,10 @@
         remote(dst, dst, swap_s.at[k, c], swap_r.at[k, c], t, partner).wait_recv()
 
     for c in range(chunks):
-        for k in range(5):
+        for k in range(4):
             later(start(swap_copy(k, c)))
+    for c in range(chunks):
+        later(start(swap_copy(4, c)))
 
     def down(f, k, c, lo, rows):
         return remote(
@@ -291,39 +297,45 @@
     def folded(value):
         return jnp.sum(value.reshape(-1, 8, nz), axis=0)
 
-    def sum_copy(e, d):
+    def each_slab(body):
+        if slabs <= 16:
+            for d in range(1, slabs):
+                body(d)
+        else:
+
+            def step(d, carry):
+                body(d)
+                return carry
+
+            lax.fori_loop(1, slabs, step, 0)
+
+    def sum_copy(m, d):
         return remote(
-            sums.at[e, s], sums.at[e, s], sum_s.at[e, d], sum_r.at[e, d],
+            sums.at[m, s], sums.at[m, s], sum_s.at[m, d], sum_r.at[m, d],
             t, lax.rem(s + d, slabs),
         )
 
-    def sum_start(e, parts):
+    def sum_start(m, parts):
         for row, part in enumerate(parts):
             flat = jnp.sum(part, axis=0, keepdims=True)
             line = flat[:, 0:128]
             for at in range(128, nz, 128):
                 line = line + flat[:, at : at + 128]
-            sums[e, s, row : row + 1, :] = line
-
-        def body(d, carry):
-            sum_copy(e, d).start()
-            return carry
-
-        lax.fori_loop(1, slabs, body, 0)
-
-    def sum_wait(e):
-        def body(d, carry):
+            sums[m, s, row : row + 1, :] = line
+        each_slab(lambda d: sum_copy(m, d).start())
+
+    def sum_wait(m):
+        def body(d):
             source = lax.rem(s - d + slabs, slabs)
             remote(
-                sums.at[e, source], sums.at[e, source], sum_s.at[e, d], sum_r.at[e, d],
+                sums.at[m, source], sums.at[m, source], sum_s.at[m, d], sum_r.at[m, d],
                 t, source,
             ).wait_recv()
-            return carry
-
-        lax.fori_loop(1, slabs, body, 0)
-        total = jnp.sum(sums[e], axis=0)
+
+        each_slab(body)
+        total = jnp.sum(sums[m], axis=0)
         total = jnp.sum(total, axis=1, keepdims=True)
-        return total[0:1, :], total[1:2, :]
+        return [total[row : row + 1, :] for row in range(4)]
 
     def halo_send(f, k, c, lo, rows):
         start(down(f, k, c, lo, rows), has_lower)
@@ -351,6 +363,8 @@
     def img_wait(m, piece):
         halo_wait(H_IMG + m, piece, *pieces_of[piece][0], (0,))
         halo_wait(H_IMG + m, piece, *pieces_of[piece][1], (1,))
+
+    nothing = jnp.zeros((8, nz), f32)
 
     def product(m):
         def body(b, carry):
@@ -360,67 +374,66 @@
             norm, along = carry
             for slab in range(2):
                 v = centre[slab]
-                z = v - WIDTHS[m] * images[slab]
-                field[IMG + m, slab, pl.ds(PAD + b, tile), :] = z
+                w = -WIDTHS[m] * images[slab]
+                field[IMG + m, slab, pl.ds(PAD + b, tile), :] = w
                 masked = jnp.where(inside, v, 0.0)
                 norm = norm + folded(masked * v)
-                along = along + folded(masked * z)
+                along = along + folded(masked * w)
             return norm, along
 
-        nothing = jnp.zeros((8, nz), f32)
-        norm, along = loop(win, tile, body, (nothing, nothing))
-        sum_start(2 * m, (norm, along))
+        sums_here = loop(win, tile, body, (nothing, nothing))
         img_send(m, 0)
+        return sums_here
 
     small = tile_of(quarter, 32)
 
-    def second(m):
-        norm_now, along = sum_wait(2 * m)
-        step_size = norm_now / along
+    def local(m):
+        def body(b, carry):
+            windows = [field[IMG + m, slab, pl.ds(b, small + 2 * PAD), :] for slab in range(2)]
+            centre, images = heat(windows, (None, None), b, small)
+            norm, along = carry
+            for slab in range(2):
+                v = centre[slab]
+                norm = norm + folded(v * v)
+                along = along + folded(v * images[slab])
+            return norm, along
+
+        return loop(half, small, body, (nothing, nothing), own)
+
+    def cross(m, sums_here, sums_local):
         img_wait(m, 0)
 
         def body_of(side):
             ref = lower if side == 0 else upper
 
             def body(b, carry):
-                windows = [
-                    field[RES + m, slab, pl.ds(b, small + 2 * PAD), :]
-                    - step_size * field[IMG + m, slab, pl.ds(b, small + 2 * PAD), :]
-                    for slab in range(2)
-                ]
-                beside = (
-                    ref[H_RES + m, pl.ds(b, small), :]
-                    - step_size * ref[H_IMG + m, pl.ds(b, small), :]
-                )
-                term = 2.0 * across[2 * side, pl.ds(b, small), :] * beside
-                outer = (term, None) if side == 0 else (None, term)
-                centre, images = heat(windows, outer, b, small)
-                norm, along = carry
-                for slab in range(2):
-                    v = centre[slab]
-                    norm = norm + folded(v * v)
-                    along = along + folded(v * (v - WIDTHS[m] * images[slab]))
-                return norm, along
+                rows = pl.ds(b, small)
+                edge = across[2 * side, rows, :] * ref[H_IMG + m, rows, :]
+                return carry + folded(edge * field[IMG + m, side, pl.ds(PAD + b, small), :])
 
             return body
 
-        nothing = jnp.zeros((8, nz), f32)
-        carry = loop(quarter, small, body_of(0), (nothing, nothing), set_up)
-        carry = loop(quarter, small, body_of(1), carry, set_down)
-        sum_start(2 * m + 1, carry)
-        return norm_now, step_size
-
-    def factors(m, norm_now, step_size):
-        norm_next, along = sum_wait(2 * m + 1)
-        momentum = norm_next / norm_now
-        step_next = norm_next / (along - momentum * norm_next / step_size)
-        return step_size + step_next * (1.0 + momentum), step_size * step_next
+        outer = loop(quarter, small, body_of(0), nothing, set_up)
+        outer = loop(quarter, small, body_of(1), outer, set_down)
+        norm, along = sums_local
+        sum_start(m, sums_here + (norm, -WIDTHS[m] * (along + 2.0 * outer)))
+
+    def factors(m):
+        rr, rw, ww, wbw = sum_wait(m)
+        step_size = rr / (rr + rw)
+        mean = rw / rr
+        square = step_size * step_size
+        norm_next = square * jnp.maximum(ww - mean * rw, 0.0)
+        along = square * jnp.maximum(mean * mean * rw - 2.0 * mean * ww + wbw, 0.0)
+        momentum = norm_next / rr
+        below = norm_next * (1.0 + momentum)
+        curve = jnp.maximum(norm_next + along - momentum * norm_next / step_size, below)
+        step_next = norm_next / jnp.maximum(curve, 1e-37)
+        on_image = step_size * step_next
+        return step_size + step_next * (1.0 + momentum) - on_image, on_image
 
     def advance(m, scalars):
         on_res, on_img = scalars
-        for c in range(chunks):
-            halo_wait(H_GAIN + m, c, *spans[c])
-        img_wait(m, 1)
 
         def body(b, carry):
             at = pl.ds(PAD + b, tile)
@@ -457,30 +470,28 @@
 
         loop(win, tile, body)
 
-    def finish(m, scalars):
+    def finish(m, scalars, slab, ref, lo, rows):
         on_res, on_img = scalars
         node = NODE + min(m, 2)
 
         def body(b, carry):
-            for slab in range(2):
-                at = pl.ds(PAD + b, small)
-                result[m, slab, pl.ds(b, small), :] = (
-                    field[node, slab, at, :]
-                    + on_res * field[RES + m, slab, at, :]
-                    - on_img * field[IMG + m, slab, at, :]
-                )
+            at = pl.ds(PAD + own + b, small)
+            ref[pl.ds(b, small), :] = (
+                field[node, slab, at, :]
+                + on_res * field[RES + m, slab, at, :]
+                - on_img * field[IMG + m, slab, at, :]
+            )
             return carry
 
-        loop(half, small, body, 0, own)
+        loop(rows, small, body, 0, lo)
 
     def residuals(b, carry):
         images = [plain_heat(NODE + j, H_NODE + j, b, tile)[1] for j in range(3)]
         at = pl.ds(PAD + b, tile)
         for slab in range(2):
             nodes = [field[NODE + j, slab, at, :] for j in range(3)]
-            ahead = [field[START, slab, at, :]] + nodes
             for row, f in enumerate((RES, GAIN, GAIN + 1)):
-                value = ahead[row] - nodes[row]
+                value = nodes[row - 1] - nodes[row] if row else -nodes[0]
                 for j in range(3):
                     value = value + (STEP * sweep_weight(row, j)) * images[j][slab]
                 field[f, slab, at, :] = value
@@ -498,165 +509,168 @@
         lo, rows = spans[c]
         loop(rows, tile, coefficients, 0, lo)
         loop(rows, tile, residuals, 0, lo)
+
+    def add_start(b, carry):
+        at = pl.ds(PAD + b, tile)
+        for slab in range(2):
+            field[RES, slab, at, :] = field[RES, slab, at, :] + field[START, slab, at, :]
+        return carry
+
+    def begin_res(c):
+        swap_wait(4, c)
+        lo, rows = spans[c]
+        loop(rows, tile, add_start, 0, lo)
         halo_send(RES, H_RES, c, lo, rows)
-        if c == 0:
-            halo_send(GAIN, H_GAIN, c, lo, rows)
-
-    order = [(k, c) for c in range(chunks) for k in range(5)]
-    ready = {}
+
     for c in range(chunks):
-        ready[min(5 * c + 6, len(order) - 1)] = c
-    for n, (k, c) in enumerate(order):
-        swap_wait(k, c)
-        if k < 4:
+        for k in range(4):
+            swap_wait(k, c)
             first_hop(k, c, other)
-        if n in ready:
-            begin_rows(ready[n])
-    for c in range(1, chunks - 1):
-        halo_send(GAIN, H_GAIN, c, *spans[c])
-
-    def give_back(m):
+        if c > 0:
+            begin_rows(c - 1)
+    for c in range(chunks):
+        if c == chunks - 1:
+            begin_rows(c)
+        begin_res(c)
+    theirs = pl.multiple_of(other * half, 8)
+
+    def mine_of(m):
+        return fine_out.at[0, m, 0, pl.ds(mine, half)]
+
+    def hand_over(m, update):
+        finish(m, update, other, result.at[m], 0, half)
+        later(start(remote(result.at[m], mine_of(m), out_s.at[m], out_r.at[m], t, partner)))
+        finish(m, update, h, mine_of(m), 0, half)
+
+    @pl.when(jnp.logical_not(has_prev))
+    def _():
+        pltpu.make_async_copy(start_in.at[0, 0], start_out.at[0, 0], copy_s.at[0]).start()
+        pltpu.make_async_copy(start_in.at[0, 0], coarse_out.at[0, 0], copy_s.at[1]).start()
+
+    def gain_send(m, chunk_range):
+        for c in chunk_range:
+            if c < chunks:
+                halo_send(GAIN + m, H_GAIN + m, c, *spans[c])
+
+    def gain_wait(m):
+        for c in range(chunks):
+            halo_wait(H_GAIN + m, c, *spans[c])
+
+    gain_send(0, range(0, 2))
+    for c in range(chunks):
+        halo_wait(H_RES, c, *spans[c])
+    here = product(0)
+    gain_send(0, range(2, 4))
+    cross(0, here, local(0))
+    gain_send(0, range(4, chunks))
+    img_send(0, 1)
+    gain_send(1, range(0, 2))
+    update = factors(0)
+    gain_wait(0)
+    img_wait(0, 1)
+    advance(0, update)
+    here = product(1)
+    gain_send(1, range(2, 4))
+    hand_over(0, update)
+    cross(1, here, local(1))
+    gain_send(1, range(4, chunks))
+    img_send(1, 1)
+    gain_wait(1)
+    coarse_residual()
+    here_coarse = product(3)
+    update = factors(1)
+    img_wait(1, 1)
+    advance(1, update)
+    here = product(2)
+    cross(3, here_coarse, local(3))
+    hand_over(1, update)
+    cross(2, here, local(2))
+
+    update = factors(3)
+    for k, slab in enumerate((other, h)):
+        finish(3, update, slab, result.at[3 + k], 0, half)
+        copy = remote(
+            result.at[3 + k], coarse_out.at[0, 0, pl.ds(mine, half)],
+            end_s.at[k], end_r.at[k], t + 1, (partner, s)[k],
+        )
+        start(copy, has_next)
+        later(copy, has_next)
+
+    pieces = 4 if half % (4 * small) == 0 else 1
+    piece = half // pieces
+
+    def pass_on(at, e):
+        copy = remote(
+            fine_out.at[0, 2, 0, pl.ds(at, piece)], start_out.at[0, 0, pl.ds(at, piece)],
+            end_s.at[e], end_r.at[e], t + 1, s,
+        )
+        start(copy, has_next)
+        later(copy, has_next)
+
+    update = factors(2)
+    for c in range(pieces):
+        finish(2, update, other, result.at[2], c * piece, piece)
         later(
             start(
                 remote(
-                    result.at[m, other, pl.ds(own, half)], fine_out.at[0, m, 0, pl.ds(mine, half)],
-                    out_s.at[m], out_r.at[m], t, partner,
-                )
-            )
-        )
-        keep = pltpu.make_async_copy(
-            result.at[m, h, pl.ds(own, half)], fine_out.at[0, m, 0, pl.ds(mine, half)], keep_s.at[m]
-        )
-        keep.start()
-        return keep
-
-    theirs = pl.multiple_of(other * half, 8)
-
-    @pl.when(jnp.logical_not(has_prev))
-    def _():
-        pltpu.make_async_copy(start_in.at[0, 0], staged, copy_s.at[0]).start()
-
-    for c in range(chunks):
-        halo_wait(H_RES, c, *spans[c])
-    product(0)
-    halo_send(GAIN, H_GAIN, chunks - 1, *spans[chunks - 1])
-    scalars = second(0)
-    img_send(0, 1)
-    halo_send(GAIN + 1, H_GAIN + 1, 0, *spans[0])
-    update = factors(0, *scalars)
-    advance(0, update)
-    product(1)
-    for c in range(1, chunks - 1):
-        halo_send(GAIN + 1, H_GAIN + 1, c, *spans[c])
-    finish(0, update)
-    keeps = [give_back(0)]
-    @pl.when(jnp.logical_not(has_prev))
-    def _():
-        pltpu.make_async_copy(start_in.at[0, 0], staged, copy_s.at[0]).wait()
-        first = pltpu.make_async_copy(staged, start_out.at[0, 0], copy_s.at[0])
-        second_copy = pltpu.make_async_copy(staged, coarse_out.at[0, 0], copy_s.at[1])
-        first.start()
-        second_copy.start()
-        first.wait()
-        second_copy.wait()
-
-    scalars = second(1)
-    img_send(1, 1)
-    halo_send(GAIN + 1, H_GAIN + 1, chunks - 1, *spans[chunks - 1])
-    update = factors(1, *scalars)
-    advance(1, update)
-    product(2)
-    coarse_residual()
-    product(3)
-    scalars = second(2)
-    finish(1, update)
-    keeps.append(give_back(1))
-    scalars_coarse = second(3)
-    finish(2, factors(2, *scalars))
-    pieces = 2
-    piece = half // pieces
-    for c in range(pieces):
-        later(
-            start(
-                remote(
-                    result.at[2, other, pl.ds(own + c * piece, piece)],
-                    mail.at[pl.ds(c * piece, piece)],
+                    result.at[2, pl.ds(c * piece, piece)],
+                    fine_out.at[0, 2, 0, pl.ds(mine + c * piece, piece)],
                     out_s.at[2 + c], out_r.at[2 + c], t, partner,
                 )
             )
         )
     for c in range(pieces):
-        rows = pl.ds(mine + c * piece, piece)
-        src = result.at[2, h, pl.ds(own + c * piece, piece)]
-        copy = remote(src, start_out.at[0, 0, rows], end_s.at[2 + c], end_r.at[2 + c], t + 1, s)
-        start(copy, has_next)
-        later(copy, has_next)
-        keep = pltpu.make_async_copy(src, fine_out.at[0, 2, 0, rows], keep_s.at[2 + c])
-        keep.start()
-        keeps.append(keep)
-    finish(3, factors(3, *scalars_coarse))
-
-    def coarse_copies():
-        return [
-            remote(
-                result.at[3, h, pl.ds(own, half)], coarse_out.at[0, 0, pl.ds(mine, half)],
-                end_s.at[0], end_r.at[0], t + 1, s,
-            ),
-            remote(
-                result.at[3, other, pl.ds(own, half)], coarse_out.at[0, 0, pl.ds(mine, half)],
-                end_s.at[1], end_r.at[1], t + 1, partner,
-            ),
-        ]
-
-    for copy in coarse_copies():
-        start(copy, has_next)
-        later(copy, has_next)
-
+        finish(2, update, h, mine_of(2), c * piece, piece)
+        pass_on(mine + c * piece, 2 + c)
     for c in range(pieces):
-        rows = pl.ds(theirs + c * piece, piece)
-        src = mail.at[pl.ds(c * piece, piece)]
+        at = theirs + c * piece
+        src = fine_out.at[0, 2, 0, pl.ds(at, piece)]
         remote(src, src, out_s.at[2 + c], out_r.at[2 + c], t, partner).wait_recv()
-        copy = remote(
-            src, start_out.at[0, 0, rows],
-            end_s.at[2 + pieces + c], end_r.at[2 + pieces + c], t + 1, s,
-        )
-        start(copy, has_next)
-        later(copy, has_next)
-        keep = pltpu.make_async_copy(src, fine_out.at[0, 2, 0, rows], keep_s.at[2 + pieces + c])
-        keep.start()
-        keeps.append(keep)
+        pass_on(at, 2 + pieces + c)
 
     for m in range(2):
         dst = fine_out.at[0, m, 0, pl.ds(theirs, half)]
         remote(dst, dst, out_s.at[m], out_r.at[m], t, partner).wait_recv()
 
+    @pl.when(jnp.logical_not(has_prev))
+    def _():
+        pltpu.make_async_copy(start_in.at[0, 0], start_out.at[0, 0], copy_s.at[0]).wait()
+        pltpu.make_async_copy(start_in.at[0, 0], coarse_out.at[0, 0], copy_s.at[1]).wait()
+
     @pl.when(has_prev)
     def _():
         for k in range(2):
-            at = mine if k == 0 else theirs
-            dst = coarse_out.at[0, 0, pl.ds(at, half)]
+            dst = coarse_out.at[0, 0, pl.ds((theirs, mine)[k], half)]
             remote(dst, dst, end_s.at[k], end_r.at[k], t - 1, s).wait_recv()
         for k in range(2):
-            at = mine if k == 0 else theirs
             for c in range(pieces):
-                dst = start_out.at[0, 0, pl.ds(at + c * piece, piece)]
+                dst = start_out.at[0, 0, pl.ds((mine, theirs)[k] + c * piece, piece)]
                 e = 2 + k * pieces + c
                 remote(dst, dst, end_s.at[e], end_r.at[e], t - 1, s).wait_recv()
 
-    for keep in keeps:
-        keep.wait()
     for copy, cond in pending:
         if cond is None:
             copy.wait_send()
         else:
             pl.when(cond)(copy.wait_send)
 
-    def drain(d, carry):
-        for e in range(8):
-            sum_copy(e, d).wait_send()
-        return carry
-
-    lax.fori_loop(1, slabs, drain, 0)
+    for m in range(4):
+        each_slab(lambda d, m=m: sum_copy(m, d).wait_send())
+
+
+def store(fine, begin, coarse, fine_out, start_out, coarse_out, sem):
+    pairs = [(begin.at[0, 0], start_out.at[0, 0]), (coarse.at[0, 0], coarse_out.at[0, 0])]
+    pairs += [(fine.at[0, m, 0], fine_out.at[0, m, 0]) for m in range(fine.shape[1])]
+    copies = []
+    for k, (src, dst) in enumerate(pairs):
+        rows = src.shape[0] // 2
+        for j in range(2):
+            at = pl.ds(j * rows, rows)
+            copies.append(pltpu.make_async_copy(src.at[at], dst.at[at], sem.at[2 * k + j]))
+    for copy in copies:
+        copy.start()
+    for copy in copies:
+        copy.wait()
 
 
 def solution(mesh):
@@ -673,35 +687,39 @@
         def body(*refs):
             kernel(slices, slabs, ny, nz, *refs)
 
-        return pl.pallas_call(
+        nodes, ends = pltpu.VMEM(old_nodes.shape, jnp.float32), pltpu.VMEM(start_value.shape, jnp.float32)
+        results = pl.pallas_call(
             body,
-            out_shape=(
-                jax.ShapeDtypeStruct(old_nodes.shape, jnp.float32),
-                jax.ShapeDtypeStruct(start_value.shape, jnp.float32),
-                jax.ShapeDtypeStruct(start_value.shape, jnp.float32),
-            ),
-            in_specs=[pl.BlockSpec(memory_space=pl.ANY)] * 3,
-            out_specs=(pl.BlockSpec(memory_space=pl.ANY),) * 3,
+            out_shape=(nodes, ends, ends),
+            in_specs=[pl.BlockSpec(memory_space=pltpu.HBM)] * 3,
+            out_specs=(pl.BlockSpec(memory_space=pltpu.VMEM),) * 3,
             scratch_shapes=[
                 vmem(FIELDS, 2, win + 2 * PAD, nz),
                 vmem(HALOS, win, nz),
                 vmem(HALOS, win, nz),
                 vmem(4, 2, win, nz),
                 vmem(3, win, nz),
-                vmem(4, 2, win, nz),
-                vmem(ny, nz),
-                vmem(half, nz),
-                vmem(8, slabs, 2, 128),
+                vmem(5, half, nz),
+                vmem(4, slabs, 4, 128),
                 dma(5, chunks), dma(5, chunks), dma(5),
                 dma(HALOS, 2, chunks), dma(HALOS, 2, chunks),
-                dma(8, slabs), dma(8, slabs),
-                dma(4), dma(4), dma(6), dma(6), dma(6), dma(2),
+                dma(4, slabs), dma(4, slabs),
+                dma(6), dma(6), dma(10), dma(10), dma(2),
             ],
             compiler_params=pltpu.CompilerParams(
-                collective_id=0, has_side_effects=True, vmem_limit_bytes=60 * 1024 * 1024
+                collective_id=0, has_side_effects=True, vmem_limit_bytes=61 * 1024 * 1024
             ),
             name="pfasst",
         )(start_value, old_nodes, diffusivity)
+        return pl.pallas_call(
+            store,
+            out_shape=tuple(jax.ShapeDtypeStruct(r.shape, jnp.float32) for r in results),
+            in_specs=[pl.BlockSpec(memory_space=pltpu.VMEM)] * 3,
+            out_specs=(pl.BlockSpec(memory_space=pltpu.HBM),) * 3,
+            scratch_shapes=[dma(4 + 2 * old_nodes.shape[1])],
+            compiler_params=pltpu.CompilerParams(vmem_limit_bytes=1024 * 1024),
+            name="store",
+        )(*results)
 
     in_specs = (
         P("tm", "space", None, None),

time: 102 us -> 93.1 us (0.913)
  the two profiles are of different devices: /device:TPU:3 before, /device:TPU:0 now
where the time goes in v1:
time: 93.1 us; the launch traced here: 91.8 us
  Pallas kernels  91.2 us (98%)
    pallas_call x1, Pallas kernels, on_device(): pl.pallas_call(body, out_shape=(nodes, ends, ends), in_specs=[pl.BlockSpe...  89.6 us

profile of v1, /device:TPU:0, one launch (start us, length us, event | category | flops | bytes accessed | tf_op | source)
XLA Modules:
  0.0 91.8 jit_solution(5108433212762488770)
XLA Ops:
  0.6 89.6 %pfasst.1 = (f32[1,3,1,512,256]{4,3,2,1,0:T(8,128)S(1)}, f32[1,1,512,256]{3,2,1,0:T(8,128)S(1)}, f32[1,1,512,256]{3,2,1,0:T(8,128)S(1)}) custom-call(f32[1,1,512,256]{3,2,1,0:T(8,128)} %refs_0_.1, f32[1,3,1,512,256]{4,3,2,1,0:T(8,128)} %refs_1_.1, f32[1,512,256]{2,1,0:T(8,128)} %refs_2_.1), custom_call_target="tpu_custom_call" | custom-call | tf_op jit(solution)/shard_map/pfasst/pallas_call | solution.py:691
  90.2 1.6 %store.1 = (f32[1,3,1,512,256]{4,3,2,1,0:T(8,128)}, f32[1,1,512,256]{3,2,1,0:T(8,128)}, f32[1,1,512,256]{3,2,1,0:T(8,128)}) custom-call(f32[1,3,1,512,256]{4,3,2,1,0:T(8,128)S(1)} %get-tuple-element.6.fine, f32[1,1,512,256]{3,2,1,0:T(8,128)S(1)} %get-tuple-element.7.begin, f32[1,1,512,256]{3,2,1,0:T(8,128)S(1)} %get-tuple-element.8.coarse), custom_call_target="tpu_custom_call" | custom-call | tf_op jit(solution)/shard_map/store/pallas_call | solution.py:714

commit v2 on v1

--- a/solution.py
+++ b/solution.py
@@ -68,8 +68,8 @@
     slices, slabs, ny, nz,
     start_in, nodes_in, kappa_in,
     fine_out, start_out, coarse_out,
-    field, lower, upper, faces, across, result, sums,
-    swap_s, swap_r, own_s, halo_s, halo_r, sum_s, sum_r, out_s, out_r, end_s, end_r, copy_s,
+    field, lower, upper, faces, across, outgoing, result, mail, sums,
+    swap_s, swap_r, own_s, kin_s, kin_r, mail_s, mail_r, halo_s, halo_r, sum_s, sum_r, out_s, out_r, end_s, end_r, copy_s,
 ):
     f32 = jnp.float32
     t = lax.axis_index("tm")
@@ -81,6 +81,8 @@
     win = half + PAD
     other = 1 - h
     partner = s + 1 - 2 * h
+    core = lax.rem(t, 2)
+    sibling = t + 1 - 2 * core
     first_row = pl.multiple_of(h * (half - PAD), 8)
     partner_row = pl.multiple_of(other * (half - PAD), 8)
     own = pl.multiple_of(PAD * h, 8)
@@ -91,15 +93,8 @@
     has_upper = p < pairs - 1
     pending = []
 
-    def start(copy, cond=None):
-        if cond is None:
-            copy.start()
-        else:
-            pl.when(cond)(copy.start)
-        return copy
-
-    def later(copy, cond=None):
-        pending.append((copy, cond))
+    def later(ref, sem, cond=None):
+        pending.append((ref, sem, cond))
 
     def remote(src, dst, send, recv, tm, space):
         return pltpu.make_async_remote_copy(
@@ -124,15 +119,13 @@
                 pl.semaphore_signal(barrier, inc=1, device_id=(tm, space), device_id_type=MESH)
 
     sources = [kappa_in.at[0]] + [nodes_in.at[0, j, 0] for j in range(3)] + [start_in.at[0, 0]]
-    loads = []
     for k, source in enumerate(sources):
-        loads.append(
-            start(
-                pltpu.make_async_copy(
-                    source.at[pl.ds(first_row, win)], field.at[k, h, pl.ds(PAD, win)], own_s.at[k]
-                )
-            )
-        )
+        pltpu.make_async_copy(
+            source.at[pl.ds(first_row, win)], field.at[k, h, pl.ds(PAD, win)], own_s.at[0]
+        ).start()
+        pltpu.make_async_copy(
+            source.at[pl.ds(partner_row, win)], outgoing.at[k], own_s.at[1]
+        ).start()
 
     zeros = jnp.zeros((PAD, nz), f32)
     for k in range(FIELDS):
@@ -165,78 +158,135 @@
     bounds = chunk_bounds(win, tile)
     chunks = len(bounds)
 
-    def swap_copy(k, c):
-        lo, rows = bounds[c]
-        return remote(
-            sources[k].at[pl.ds(partner_row + lo, rows)],
-            field.at[k, h, pl.ds(PAD + lo, rows)],
-            swap_s.at[k, c], swap_r.at[k, c], t, partner,
-        )
+    cuts = [8 * (win // 8 * q // 4) for q in range(5)]
+    parts = [(cuts[q], cuts[q + 1] - cuts[q]) for q in range(4)]
+    share = slices % 2 == 0
+
+    def bounds_of(k, c):
+        return bounds[c] if k else parts[c]
+
+    def each_part(body):
+        for q in range(4):
+            if share:
+                pl.when(core == q // 2)(lambda q=q: body(q))
+            else:
+                body(q)
+
+    halves = [(cuts[0], cuts[2]), (cuts[2], cuts[4] - cuts[2])] if share else [(0, win)]
+
+    def each_half(body, mine_too=True):
+        for q, (lo, rows) in enumerate(halves):
+            if share:
+                pl.when((core == q) == mine_too)(lambda lo=lo, rows=rows: body(lo, rows))
+            else:
+                body(lo, rows)
+
+    def arrived(ref, sem):
+        remote(ref, ref, sum_s.at[0], sem, t, partner).wait_recv()
+
+    def sent(ref, sem):
+        remote(ref, ref, sem, sum_r.at[0], t, partner).wait_send()
+
+    def swap_sem(k, c):
+        return swap_r.at[4 + (k - 1) * chunks + c if k else c]
+
+    def swap_start(k, c):
+        lo, rows = bounds_of(k, c)
+        remote(
+            outgoing.at[k, pl.ds(lo, rows)], field.at[k, h, pl.ds(PAD + lo, rows)],
+            swap_s.at[min(k, 1)], swap_sem(k, c), t, partner,
+        ).start()
 
     def swap_wait(k, c):
-        lo, rows = bounds[c]
-        dst = field.at[k, other, pl.ds(PAD + lo, rows)]
-        remote(dst, dst, swap_s.at[k, c], swap_r.at[k, c], t, partner).wait_recv()
-
+        lo, rows = bounds_of(k, c)
+        arrived(field.at[k, other, pl.ds(PAD + lo, rows)], swap_sem(k, c))
+
+    def kin_ref(e, lo, rows):
+        if e == 0:
+            return field.at[KAPPA, other, pl.ds(PAD + lo, rows)]
+        return (lower, upper)[e - 1].at[H_KAPPA, pl.ds(lo, rows)]
+
+    def kin_copy(e, lo, rows):
+        ref = kin_ref(e, lo, rows)
+        return remote(ref, ref, kin_s.at[e], kin_r.at[e], sibling, s)
+
+    def kin_start(e):
+        if share:
+            each_half(lambda lo, rows: kin_copy(e, lo, rows).start())
+
+    def kin_wait(e):
+        if share:
+            each_half(lambda lo, rows: arrived(kin_ref(e, lo, rows), kin_r.at[e]), False)
+
+    def kin_sent(e):
+        if share:
+            each_half(lambda lo, rows: sent(kin_ref(e, lo, rows), kin_s.at[e]))
+
+    pltpu.make_async_copy(outgoing, outgoing, own_s.at[1]).wait()
+    each_part(lambda q: swap_start(0, q))
     for c in range(chunks):
-        for k in range(4):
-            later(start(swap_copy(k, c)))
+        for k in range(1, 4):
+            swap_start(k, c)
     for c in range(chunks):
-        later(start(swap_copy(4, c)))
+        swap_start(4, c)
+    later(outgoing.at[pl.ds(1, 4)], swap_s.at[1])
+
+    def halo_sems(k, c, side):
+        if k == H_KAPPA:
+            slots = 0, 0
+        elif k < H_RES:
+            slots = 1, 1 + c
+        elif k == H_RES:
+            slots = 2, 1 + chunks
+        elif k >= H_GAIN:
+            slots = 3, 2 + chunks + k - H_GAIN
+        else:
+            m = k - H_IMG
+            slots = 4 + m // 2, 4 + chunks + (2 * m + c if m < 2 else 2 + m)
+        return halo_s.at[side, slots[0]], halo_r.at[side, slots[1]]
 
     def down(f, k, c, lo, rows):
         return remote(
             field.at[f, 0, pl.ds(PAD + lo, rows)], upper.at[k, pl.ds(lo, rows)],
-            halo_s.at[k, 0, c], halo_r.at[k, 0, c], t, s - 2,
+            *halo_sems(k, c, 0), t, s - 2,
         )
 
     def up(f, k, c, lo, rows):
         return remote(
             field.at[f, 1, pl.ds(PAD + lo, rows)], lower.at[k, pl.ds(lo, rows)],
-            halo_s.at[k, 1, c], halo_r.at[k, 1, c], t, s + 2,
+            *halo_sems(k, c, 1), t, s + 2,
         )
 
     def first_hop(k, c, which):
         @pl.when(jnp.logical_and(which == 0, has_lower))
         def _():
-            down(k, k, c, *bounds[c]).start()
+            down(k, k, c, *bounds_of(k, c)).start()
 
         @pl.when(jnp.logical_and(which == 1, has_upper))
         def _():
-            up(k, k, c, *bounds[c]).start()
-
-    for copy in loads:
-        copy.wait()
+            up(k, k, c, *bounds_of(k, c)).start()
+
+    own_rows = field.at[pl.ds(0, 5), h, pl.ds(PAD, win)]
+    pltpu.make_async_copy(own_rows, own_rows, own_s.at[0]).wait()
+    each_part(lambda q: first_hop(0, q, h))
     for c in range(chunks):
-        for k in range(4):
+        for k in range(1, 4):
             first_hop(k, c, h)
 
-    def halo_wait(k, c, lo, rows, sides=(0, 1)):
-        if 0 in sides:
-
-            @pl.when(has_upper)
-            def _():
-                remote(
-                    upper.at[k, pl.ds(lo, rows)], upper.at[k, pl.ds(lo, rows)],
-                    halo_s.at[k, 0, c], halo_r.at[k, 0, c], t, s + 2,
-                ).wait_recv()
-
-        if 1 in sides:
-
-            @pl.when(has_lower)
-            def _():
-                remote(
-                    lower.at[k, pl.ds(lo, rows)], lower.at[k, pl.ds(lo, rows)],
-                    halo_s.at[k, 1, c], halo_r.at[k, 1, c], t, s - 2,
-                ).wait_recv()
-
-    def halo_sent(f, k, c, lo, rows):
-        later(down(f, k, c, lo, rows), has_lower)
-        later(up(f, k, c, lo, rows), has_upper)
-
-    for k in range(4):
-        for c in range(chunks):
-            halo_sent(k, k, c, *bounds[c])
+    def halo_wait(k, c, lo, rows, sides=(0, 1), fields=None):
+        which = k if fields is None else pl.ds(k, fields)
+        for side, ref, cond in ((0, upper, has_upper), (1, lower, has_lower)):
+            if side in sides:
+
+                @pl.when(cond)
+                def _(side=side, ref=ref):
+                    arrived(ref.at[which, pl.ds(lo, rows)], halo_sems(k, c, side)[1])
+
+    def halo_later(f, slot, lo, rows, fields=None, sides=(0, 1)):
+        which = f if fields is None else pl.ds(f, fields)
+        for side in sides:
+            ref = field.at[which, side, pl.ds(PAD + lo, rows)]
+            later(ref, halo_s.at[side, slot], (has_lower, has_upper)[side])
 
     lane = lax.broadcasted_iota(jnp.int32, (tile, nz), 1)
 
@@ -311,8 +361,7 @@
 
     def sum_copy(m, d):
         return remote(
-            sums.at[m, s], sums.at[m, s], sum_s.at[m, d], sum_r.at[m, d],
-            t, lax.rem(s + d, slabs),
+            sums.at[m, s], sums.at[m, s], sum_s.at[0], sum_r.at[m], t, lax.rem(s + d, slabs),
         )
 
     def sum_start(m, parts):
@@ -325,22 +374,14 @@
         each_slab(lambda d: sum_copy(m, d).start())
 
     def sum_wait(m):
-        def body(d):
-            source = lax.rem(s - d + slabs, slabs)
-            remote(
-                sums.at[m, source], sums.at[m, source], sum_s.at[m, d], sum_r.at[m, d],
-                t, source,
-            ).wait_recv()
-
-        each_slab(body)
+        arrived(sums.at[m, pl.ds(0, slabs - 1)], sum_r.at[m])
         total = jnp.sum(sums[m], axis=0)
         total = jnp.sum(total, axis=1, keepdims=True)
         return [total[row : row + 1, :] for row in range(4)]
 
     def halo_send(f, k, c, lo, rows):
-        start(down(f, k, c, lo, rows), has_lower)
-        start(up(f, k, c, lo, rows), has_upper)
-        halo_sent(f, k, c, lo, rows)
+        pl.when(has_lower)(down(f, k, c, lo, rows).start)
+        pl.when(has_upper)(up(f, k, c, lo, rows).start)
 
     quarter = half // 2
     set_up = own
@@ -352,13 +393,8 @@
 
     def img_send(m, piece):
         (lo_d, rows_d), (lo_u, rows_u) = pieces_of[piece]
-        copies = (
-            (down(IMG + m, H_IMG + m, piece, lo_d, rows_d), has_lower),
-            (up(IMG + m, H_IMG + m, piece, lo_u, rows_u), has_upper),
-        )
-        for copy, cond in copies:
-            start(copy, cond)
-            later(copy, cond)
+        pl.when(has_lower)(down(IMG + m, H_IMG + m, piece, lo_d, rows_d).start)
+        pl.when(has_upper)(up(IMG + m, H_IMG + m, piece, lo_u, rows_u).start)
 
     def img_wait(m, piece):
         halo_wait(H_IMG + m, piece, *pieces_of[piece][0], (0,))
@@ -457,11 +493,17 @@
     def coarse_residual():
         def body(b, carry):
             at = pl.ds(PAD + b, tile)
-            rows = pl.ds(b, tile)
             for slab in range(2):
                 field[RES + 3, slab, at, :] = (
                     field[RES, slab, at, :] + field[GAIN, slab, at, :] + field[GAIN + 1, slab, at, :]
                 )
+            return carry
+
+        loop(win, tile, body)
+
+    def coarse_halo():
+        def body(b, carry):
+            rows = pl.ds(b, tile)
             for ref in (lower, upper):
                 ref[H_RES + 3, rows, :] = (
                     ref[H_RES, rows, :] + ref[H_GAIN, rows, :] + ref[H_GAIN + 1, rows, :]
@@ -469,6 +511,19 @@
             return carry
 
         loop(win, tile, body)
+
+    def mail_copy(k):
+        return remote(
+            field.at[(RES + 3, IMG + 3)[k], other, pl.ds(PAD + own, half)], mail.at[k],
+            mail_s.at[k], mail_r.at[k], t, partner,
+        )
+
+    def mail_send(k):
+        pl.when(has_next)(mail_copy(k).start)
+        later(mail.at[k], mail_s.at[k], has_next)
+
+    def mail_wait(k):
+        pl.when(has_next)(mail_copy(k).wait_recv)
 
     def finish(m, scalars, slab, ref, lo, rows):
         on_res, on_img = scalars
@@ -504,8 +559,7 @@
         spans.append((begin, end - begin))
 
     def begin_rows(c):
-        for k in range(4):
-            halo_wait(k, c, *bounds[c])
+        halo_wait(H_NODE, c, *bounds[c], fields=3)
         lo, rows = spans[c]
         loop(rows, tile, coefficients, 0, lo)
         loop(rows, tile, residuals, 0, lo)
@@ -522,10 +576,25 @@
         loop(rows, tile, add_start, 0, lo)
         halo_send(RES, H_RES, c, lo, rows)
 
+    def pass_kappa(q):
+        swap_wait(0, q)
+        if share:
+            kin_copy(0, *parts[q]).start()
+        first_hop(0, q, other)
+
+    each_part(pass_kappa)
     for c in range(chunks):
-        for k in range(4):
+        for k in range(1, 4):
             swap_wait(k, c)
             first_hop(k, c, other)
+        if c == 0:
+            each_half(lambda lo, rows: halo_wait(H_KAPPA, 0, lo, rows))
+            pl.when(has_lower)(lambda: kin_start(1))
+            pl.when(has_upper)(lambda: kin_start(2))
+        if c == min(1, chunks - 1):
+            kin_wait(0)
+            pl.when(has_lower)(lambda: kin_wait(1))
+            pl.when(has_upper)(lambda: kin_wait(2))
         if c > 0:
             begin_rows(c - 1)
     for c in range(chunks):
@@ -539,7 +608,8 @@
 
     def hand_over(m, update):
         finish(m, update, other, result.at[m], 0, half)
-        later(start(remote(result.at[m], mine_of(m), out_s.at[m], out_r.at[m], t, partner)))
+        remote(result.at[m], mine_of(m), out_s.at[m], out_r.at[m], t, partner).start()
+        later(result.at[m], out_s.at[m])
         finish(m, update, h, mine_of(m), 0, half)
 
     @pl.when(jnp.logical_not(has_prev))
@@ -553,84 +623,95 @@
                 halo_send(GAIN + m, H_GAIN + m, c, *spans[c])
 
     def gain_wait(m):
-        for c in range(chunks):
-            halo_wait(H_GAIN + m, c, *spans[c])
+        halo_wait(H_GAIN + m, 0, 0, win)
 
     gain_send(0, range(0, 2))
-    for c in range(chunks):
-        halo_wait(H_RES, c, *spans[c])
+    halo_wait(H_RES, 0, 0, win)
     here = product(0)
     gain_send(0, range(2, 4))
     cross(0, here, local(0))
     gain_send(0, range(4, chunks))
     img_send(0, 1)
     gain_send(1, range(0, 2))
+    coarse_residual()
+    mail_send(0)
     update = factors(0)
     gain_wait(0)
     img_wait(0, 1)
     advance(0, update)
     here = product(1)
     gain_send(1, range(2, 4))
+    cross(1, here, local(1))
     hand_over(0, update)
-    cross(1, here, local(1))
     gain_send(1, range(4, chunks))
     img_send(1, 1)
     gain_wait(1)
-    coarse_residual()
+    coarse_halo()
     here_coarse = product(3)
+    mail_send(1)
     update = factors(1)
     img_wait(1, 1)
     advance(1, update)
     here = product(2)
     cross(3, here_coarse, local(3))
+    cross(2, here, local(2))
     hand_over(1, update)
-    cross(2, here, local(2))
+
+    def coarse_send(k):
+        copy = remote(
+            result.at[3 + k], coarse_out.at[0, 0, pl.ds((mine, theirs)[k], half)],
+            end_s.at[0], end_r.at[0], t + 1, s,
+        )
+        pl.when(has_next)(copy.start)
 
     update = factors(3)
-    for k, slab in enumerate((other, h)):
-        finish(3, update, slab, result.at[3 + k], 0, half)
-        copy = remote(
-            result.at[3 + k], coarse_out.at[0, 0, pl.ds(mine, half)],
-            end_s.at[k], end_r.at[k], t + 1, (partner, s)[k],
-        )
-        start(copy, has_next)
-        later(copy, has_next)
+    finish(3, update, h, result.at[3], 0, half)
+    coarse_send(0)
+    for k in range(2):
+        mail_wait(k)
+
+    def coarse_rest(b, carry):
+        rows = pl.ds(b, small)
+        result[4, rows, :] = (
+            outgoing[3, pl.ds(PAD * other + b, small), :]
+            + update[0] * mail[0, rows, :]
+            - update[1] * mail[1, rows, :]
+        )
+        return carry
+
+    loop(half, small, coarse_rest)
+    coarse_send(1)
 
     pieces = 4 if half % (4 * small) == 0 else 1
     piece = half // pieces
 
-    def pass_on(at, e):
+    def pass_on(at):
         copy = remote(
             fine_out.at[0, 2, 0, pl.ds(at, piece)], start_out.at[0, 0, pl.ds(at, piece)],
-            end_s.at[e], end_r.at[e], t + 1, s,
-        )
-        start(copy, has_next)
-        later(copy, has_next)
+            end_s.at[1], end_r.at[1], t + 1, s,
+        )
+        pl.when(has_next)(copy.start)
 
     update = factors(2)
     for c in range(pieces):
         finish(2, update, other, result.at[2], c * piece, piece)
-        later(
-            start(
-                remote(
-                    result.at[2, pl.ds(c * piece, piece)],
-                    fine_out.at[0, 2, 0, pl.ds(mine + c * piece, piece)],
-                    out_s.at[2 + c], out_r.at[2 + c], t, partner,
-                )
-            )
-        )
+        remote(
+            result.at[2, pl.ds(c * piece, piece)],
+            fine_out.at[0, 2, 0, pl.ds(mine + c * piece, piece)],
+            out_s.at[2], out_r.at[2 + c], t, partner,
+        ).start()
     for c in range(pieces):
         finish(2, update, h, mine_of(2), c * piece, piece)
-        pass_on(mine + c * piece, 2 + c)
+        pass_on(mine + c * piece)
     for c in range(pieces):
         at = theirs + c * piece
         src = fine_out.at[0, 2, 0, pl.ds(at, piece)]
-        remote(src, src, out_s.at[2 + c], out_r.at[2 + c], t, partner).wait_recv()
-        pass_on(at, 2 + pieces + c)
+        arrived(src, out_r.at[2 + c])
+        pass_on(at)
 
     for m in range(2):
         dst = fine_out.at[0, m, 0, pl.ds(theirs, half)]
-        remote(dst, dst, out_s.at[m], out_r.at[m], t, partner).wait_recv()
+        arrived(dst, out_r.at[m])
 
     @pl.when(jnp.logical_not(has_prev))
     def _():
@@ -639,23 +720,38 @@
 
     @pl.when(has_prev)
     def _():
-        for k in range(2):
-            dst = coarse_out.at[0, 0, pl.ds((theirs, mine)[k], half)]
-            remote(dst, dst, end_s.at[k], end_r.at[k], t - 1, s).wait_recv()
-        for k in range(2):
-            for c in range(pieces):
-                dst = start_out.at[0, 0, pl.ds((mine, theirs)[k] + c * piece, piece)]
-                e = 2 + k * pieces + c
-                remote(dst, dst, end_s.at[e], end_r.at[e], t - 1, s).wait_recv()
-
-    for copy, cond in pending:
+        arrived(coarse_out.at[0, 0], end_r.at[0])
+        arrived(start_out.at[0, 0], end_r.at[1])
+
+    each_half(lambda lo, rows: sent(outgoing.at[0, pl.ds(lo, rows)], swap_s.at[0]))
+    for side, cond in ((0, has_lower), (1, has_upper)):
+
+        @pl.when(cond)
+        def _(side=side):
+            each_half(
+                lambda lo, rows: sent(
+                    field.at[KAPPA, side, pl.ds(PAD + lo, rows)], halo_s.at[side, 0]
+                )
+            )
+
+    kin_sent(0)
+    pl.when(has_lower)(lambda: kin_sent(1))
+    pl.when(has_upper)(lambda: kin_sent(2))
+    halo_later(NODE, 1, 0, win, 3)
+    halo_later(RES, 2, 0, win)
+    halo_later(GAIN, 3, 0, win, 2)
+    halo_later(IMG, 4, 0, win, 2)
+    for side in range(2):
+        halo_later(IMG + 2, 5, *pieces_of[0][side], 2, (side,))
+    later(result.at[2], out_s.at[2])
+    later(result.at[pl.ds(3, 2)], end_s.at[0], has_next)
+    later(fine_out.at[0, 2, 0], end_s.at[1], has_next)
+    later(sums.at[pl.ds(0, 4), pl.ds(0, slabs - 1)], sum_s.at[0])
+    for ref, sem, cond in pending:
         if cond is None:
-            copy.wait_send()
+            sent(ref, sem)
         else:
-            pl.when(cond)(copy.wait_send)
-
-    for m in range(4):
-        each_slab(lambda d, m=m: sum_copy(m, d).wait_send())
+            pl.when(cond)(lambda ref=ref, sem=sem: sent(ref, sem))
 
 
 def store(fine, begin, coarse, fine_out, start_out, coarse_out, sem):
@@ -699,12 +795,13 @@
                 vmem(HALOS, win, nz),
                 vmem(4, 2, win, nz),
                 vmem(3, win, nz),
+                vmem(5, win, nz),
                 vmem(5, half, nz),
+                vmem(2, half, nz),
                 vmem(4, slabs, 4, 128),
-                dma(5, chunks), dma(5, chunks), dma(5),
-                dma(HALOS, 2, chunks), dma(HALOS, 2, chunks),
-                dma(4, slabs), dma(4, slabs),
-                dma(6), dma(6), dma(10), dma(10), dma(2),
+                dma(2), dma(4 + 4 * chunks), dma(2), dma(3), dma(3), dma(2), dma(2),
+                dma(2, 6), dma(2, 10 + chunks), dma(1), dma(4),
+                dma(3), dma(6), dma(2), dma(2), dma(2),
             ],
             compiler_params=pltpu.CompilerParams(
                 collective_id=0, has_side_effects=True, vmem_limit_bytes=61 * 1024 * 1024

time: 93.1 us -> 85.3 us (0.916); the launches traced: 91.8 us -> 85.1 us
  Pallas kernels: 91.2 us -> 84.5 us
    pallas_call x1, Pallas kernels: 89.6 us -> 82.9 us  [on_device(): pl.pallas_call(body, out_shape=(nodes, ends, ends), in_specs=[pl.BlockSpe...]
where the time goes in v2:
time: 85.3 us; the launch traced here: 85.1 us
  Pallas kernels  84.5 us (99%)
    pallas_call x1, Pallas kernels, on_device(): pl.pallas_call(body, out_shape=(nodes, ends, ends), in_specs=[pl.BlockSpe...  82.9 us

profile of v2, /device:TPU:0, one launch (start us, length us, event | category | flops | bytes accessed | tf_op | source)
XLA Modules:
  0.0 85.1 jit_solution(819882303691745323)
XLA Ops:
  0.6 82.9 %pfasst.1 = (f32[1,3,1,512,256]{4,3,2,1,0:T(8,128)S(1)}, f32[1,1,512,256]{3,2,1,0:T(8,128)S(1)}, f32[1,1,512,256]{3,2,1,0:T(8,128)S(1)}) custom-call(f32[1,1,512,256]{3,2,1,0:T(8,128)} %refs_0_.1, f32[1,3,1,512,256]{4,3,2,1,0:T(8,128)} %refs_1_.1, f32[1,512,256]{2,1,0:T(8,128)} %refs_2_.1), custom_call_target="tpu_custom_call" | custom-call | tf_op jit(solution)/shard_map/pfasst/pallas_call | solution.py:787
  83.5 1.6 %store.1 = (f32[1,3,1,512,256]{4,3,2,1,0:T(8,128)}, f32[1,1,512,256]{3,2,1,0:T(8,128)}, f32[1,1,512,256]{3,2,1,0:T(8,128)}) custom-call(f32[1,3,1,512,256]{4,3,2,1,0:T(8,128)S(1)} %get-tuple-element.6.fine, f32[1,1,512,256]{3,2,1,0:T(8,128)S(1)} %get-tuple-element.7.begin, f32[1,1,512,256]{3,2,1,0:T(8,128)S(1)} %get-tuple-element.8.coarse), custom_call_target="tpu_custom_call" | custom-call | tf_op jit(solution)/shard_map/store/pallas_call | solution.py:811

commit v3 on v2

--- a/solution.py
+++ b/solution.py
@@ -25,6 +25,7 @@
 ]
 MESH = pl.DeviceIdType.MESH
 PAD = 8
+SOUTH_PARTS = 2
 
 KAPPA, NODE, START, RES, IMG, GAIN = 0, 1, 4, 5, 9, 13
 FIELDS = 15
@@ -68,8 +69,8 @@
     slices, slabs, ny, nz,
     start_in, nodes_in, kappa_in,
     fine_out, start_out, coarse_out,
-    field, lower, upper, faces, across, outgoing, result, mail, sums,
-    swap_s, swap_r, own_s, kin_s, kin_r, mail_s, mail_r, halo_s, halo_r, sum_s, sum_r, out_s, out_r, end_s, end_r, copy_s,
+    field, lower, upper, faces, across, outgoing, result, mail, kept, marks, sums,
+    swap_s, swap_r, own_s, kin_s, kin_r, mail_s, mail_r, kept_s, kept_r, halo_s, halo_r, sum_s, sum_r, out_s, out_r, end_s, end_r, copy_s,
 ):
     f32 = jnp.float32
     t = lax.axis_index("tm")
@@ -168,17 +169,18 @@
     def each_part(body):
         for q in range(4):
             if share:
-                pl.when(core == q // 2)(lambda q=q: body(q))
+                pl.when(core == (q >= SOUTH_PARTS))(lambda q=q: body(q))
             else:
                 body(q)
 
-    halves = [(cuts[0], cuts[2]), (cuts[2], cuts[4] - cuts[2])] if share else [(0, win)]
+    first = cuts[SOUTH_PARTS]
+    halves = [(0, first), (first, win - first)] if share else [(0, win)]
 
     def each_half(body, mine_too=True):
         for q, (lo, rows) in enumerate(halves):
-            if share:
+            if share and rows:
                 pl.when((core == q) == mine_too)(lambda lo=lo, rows=rows: body(lo, rows))
-            else:
+            elif not share:
                 body(lo, rows)
 
     def arrived(ref, sem):
@@ -512,18 +514,32 @@
 
         loop(win, tile, body)
 
+    mailed = (GAIN, GAIN + 1, IMG + 1, IMG + 2)
+
     def mail_copy(k):
         return remote(
-            field.at[(RES + 3, IMG + 3)[k], other, pl.ds(PAD + own, half)], mail.at[k],
+            field.at[mailed[k], other, pl.ds(PAD + own, half)], mail.at[k],
             mail_s.at[k], mail_r.at[k], t, partner,
         )
 
     def mail_send(k):
-        pl.when(has_next)(mail_copy(k).start)
-        later(mail.at[k], mail_s.at[k], has_next)
-
-    def mail_wait(k):
-        pl.when(has_next)(mail_copy(k).wait_recv)
+        mail_copy(k).start()
+        later(mail.at[k], mail_s.at[k])
+
+    def coarse_send(k, which=(0, 1)):
+        for slab, space in [((h, s), (other, partner))[w] for w in which]:
+            copy = remote(
+                field.at[(RES + 3, IMG + 3)[k - 1], slab, pl.ds(PAD + own, half)],
+                kept.at[k, pl.ds(mine, half)], kept_s.at[k], kept_r.at[k], t + 1, space,
+            )
+            pl.when(has_next)(copy.start)
+
+    def kept_copy(k):
+        if k == 0:
+            src, dst = nodes_in.at[0, 2, 0], kept.at[0]
+        else:
+            src, dst = marks.at[0], marks.at[1]
+        return remote(src, dst, kept_s.at[k], kept_r.at[k], t + 1, s)
 
     def finish(m, scalars, slab, ref, lo, rows):
         on_res, on_img = scalars
@@ -601,16 +617,62 @@
         if c == chunks - 1:
             begin_rows(c)
         begin_res(c)
+    mail_send(0)
+    mail_send(1)
     theirs = pl.multiple_of(other * half, 8)
-
-    def mine_of(m):
-        return fine_out.at[0, m, 0, pl.ds(mine, half)]
-
-    def hand_over(m, update):
-        finish(m, update, other, result.at[m], 0, half)
-        remote(result.at[m], mine_of(m), out_s.at[m], out_r.at[m], t, partner).start()
-        later(result.at[m], out_s.at[m])
-        finish(m, update, h, mine_of(m), 0, half)
+    beside = pl.multiple_of(PAD * other, 8)
+
+    def half_of(m, at):
+        return fine_out.at[0, m, 0, pl.ds(at, half)]
+
+    def finish_start(update):
+        finish(0, update, other, result, 0, half)
+        remote(result, half_of(0, mine), out_s.at[0], out_r.at[0], t, partner).start()
+        later(result, out_s.at[0])
+        finish(0, update, h, half_of(0, mine), 0, half)
+
+    def finish_second(update):
+        finish(1, update, h, half_of(1, mine), 0, half)
+        arrived(half_of(0, theirs), out_r.at[0])
+        for k in range(3):
+            mail_copy(k).wait_recv()
+
+        def body(b, carry):
+            rows, at = pl.ds(b, small), pl.ds(beside + b, small)
+            there = pl.ds(theirs + b, small)
+            residual = fine_out[0, 0, 0, there, :] - outgoing[1, at, :] + mail[0, rows, :]
+            step = update[0] * residual - update[1] * mail[2, rows, :]
+            fine_out[0, 1, 0, there, :] = outgoing[2, at, :] + step
+            mail[1, rows, :] = mail[1, rows, :] + step
+            return carry
+
+        loop(half, small, body)
+
+    def finish_third(update, lo, rows):
+        def body(b, carry):
+            at = pl.ds(b, small)
+            fine_out[0, 2, 0, pl.ds(theirs + b, small), :] = (
+                outgoing[3, pl.ds(beside + b, small), :]
+                + update[0] * mail[1, at, :]
+                - update[1] * mail[3, at, :]
+            )
+            return carry
+
+        loop(rows, small, body, 0, lo)
+
+    def finish_coarse():
+        on_res, on_img = marks[1, 0:1, 0:1], marks[1, 1:2, 0:1]
+
+        def body(b, carry):
+            at = pl.ds(b, small)
+            coarse_out[0, 0, at, :] = (
+                kept[0, at, :] + on_res * kept[1, at, :] - on_img * kept[2, at, :]
+            )
+            return carry
+
+        loop(ny, small, body)
+
+    pl.when(has_next)(kept_copy(0).start)
 
     @pl.when(jnp.logical_not(has_prev))
     def _():
@@ -634,84 +696,55 @@
     img_send(0, 1)
     gain_send(1, range(0, 2))
     coarse_residual()
-    mail_send(0)
+    coarse_send(1)
     update = factors(0)
     gain_wait(0)
     img_wait(0, 1)
     advance(0, update)
     here = product(1)
+    mail_send(2)
     gain_send(1, range(2, 4))
     cross(1, here, local(1))
-    hand_over(0, update)
+    finish_start(update)
     gain_send(1, range(4, chunks))
     img_send(1, 1)
     gain_wait(1)
     coarse_halo()
     here_coarse = product(3)
-    mail_send(1)
+    coarse_send(2, (0,))
     update = factors(1)
     img_wait(1, 1)
     advance(1, update)
     here = product(2)
+    mail_send(3)
     cross(3, here_coarse, local(3))
     cross(2, here, local(2))
-    hand_over(1, update)
-
-    def coarse_send(k):
+    coarse_send(2, (1,))
+    finish_second(update)
+
+    pieces = 2 if half % (2 * small) == 0 else 1
+    piece = half // pieces
+
+    def pass_on(at):
         copy = remote(
-            result.at[3 + k], coarse_out.at[0, 0, pl.ds((mine, theirs)[k], half)],
+            fine_out.at[0, 2, 0, pl.ds(at, piece)], start_out.at[0, 0, pl.ds(at, piece)],
             end_s.at[0], end_r.at[0], t + 1, s,
         )
         pl.when(has_next)(copy.start)
 
     update = factors(3)
-    finish(3, update, h, result.at[3], 0, half)
-    coarse_send(0)
-    for k in range(2):
-        mail_wait(k)
-
-    def coarse_rest(b, carry):
-        rows = pl.ds(b, small)
-        result[4, rows, :] = (
-            outgoing[3, pl.ds(PAD * other + b, small), :]
-            + update[0] * mail[0, rows, :]
-            - update[1] * mail[1, rows, :]
-        )
-        return carry
-
-    loop(half, small, coarse_rest)
-    coarse_send(1)
-
-    pieces = 4 if half % (4 * small) == 0 else 1
-    piece = half // pieces
-
-    def pass_on(at):
-        copy = remote(
-            fine_out.at[0, 2, 0, pl.ds(at, piece)], start_out.at[0, 0, pl.ds(at, piece)],
-            end_s.at[1], end_r.at[1], t + 1, s,
-        )
-        pl.when(has_next)(copy.start)
-
+    for row in range(2):
+        marks[0, row : row + 1, :] = jnp.broadcast_to(update[row], (1, 128))
+    pl.when(has_next)(kept_copy(3).start)
+
+    mail_copy(3).wait_recv()
     update = factors(2)
     for c in range(pieces):
-        finish(2, update, other, result.at[2], c * piece, piece)
-        remote(
-            result.at[2, pl.ds(c * piece, piece)],
-            fine_out.at[0, 2, 0, pl.ds(mine + c * piece, piece)],
-            out_s.at[2], out_r.at[2 + c], t, partner,
-        ).start()
-    for c in range(pieces):
-        finish(2, update, h, mine_of(2), c * piece, piece)
+        finish(2, update, h, half_of(2, mine), c * piece, piece)
         pass_on(mine + c * piece)
     for c in range(pieces):
-        at = theirs + c * piece
-        src = fine_out.at[0, 2, 0, pl.ds(at, piece)]
-        arrived(src, out_r.at[2 + c])
-        pass_on(at)
-
-    for m in range(2):
-        dst = fine_out.at[0, m, 0, pl.ds(theirs, half)]
-        arrived(dst, out_r.at[m])
+        finish_third(update, c * piece, piece)
+        pass_on(theirs + c * piece)
 
     @pl.when(jnp.logical_not(has_prev))
     def _():
@@ -720,8 +753,11 @@
 
     @pl.when(has_prev)
     def _():
-        arrived(coarse_out.at[0, 0], end_r.at[0])
-        arrived(start_out.at[0, 0], end_r.at[1])
+        for k in range(3):
+            arrived(kept.at[k], kept_r.at[k])
+        arrived(marks.at[1], kept_r.at[3])
+        finish_coarse()
+        arrived(start_out.at[0, 0], end_r.at[0])
 
     each_half(lambda lo, rows: sent(outgoing.at[0, pl.ds(lo, rows)], swap_s.at[0]))
     for side, cond in ((0, has_lower), (1, has_upper)):
@@ -743,9 +779,10 @@
     halo_later(IMG, 4, 0, win, 2)
     for side in range(2):
         halo_later(IMG + 2, 5, *pieces_of[0][side], 2, (side,))
-    later(result.at[2], out_s.at[2])
-    later(result.at[pl.ds(3, 2)], end_s.at[0], has_next)
-    later(fine_out.at[0, 2, 0], end_s.at[1], has_next)
+    for k in range(3):
+        later(kept.at[k], kept_s.at[k], has_next)
+    later(marks.at[0], kept_s.at[3], has_next)
+    later(fine_out.at[0, 2, 0], end_s.at[0], has_next)
     later(sums.at[pl.ds(0, 4), pl.ds(0, slabs - 1)], sum_s.at[0])
     for ref, sem, cond in pending:
         if cond is None:
@@ -796,12 +833,14 @@
                 vmem(4, 2, win, nz),
                 vmem(3, win, nz),
                 vmem(5, win, nz),
-                vmem(5, half, nz),
-                vmem(2, half, nz),
+                vmem(half, nz),
+                vmem(4, half, nz),
+                vmem(3, ny, nz),
+                vmem(2, 8, 128),
                 vmem(4, slabs, 4, 128),
-                dma(2), dma(4 + 4 * chunks), dma(2), dma(3), dma(3), dma(2), dma(2),
+                dma(2), dma(4 + 4 * chunks), dma(2), dma(3), dma(3), dma(4), dma(4), dma(4), dma(4),
                 dma(2, 6), dma(2, 10 + chunks), dma(1), dma(4),
-                dma(3), dma(6), dma(2), dma(2), dma(2),
+                dma(1), dma(1), dma(1), dma(1), dma(2),
             ],
             compiler_params=pltpu.CompilerParams(
                 collective_id=0, has_side_effects=True, vmem_limit_bytes=61 * 1024 * 1024

time: 85.3 us -> 79.6 us (0.933)
  Pallas kernels: 84.5 us -> 78.8 us
    pallas_call x1, Pallas kernels: 82.9 us -> 77.2 us  [on_device(): pl.pallas_call(body, out_shape=(nodes, ends, ends), in_specs=[pl.BlockSpe...]
where the time goes in v3:
time: 79.6 us; the launch traced here: 79.4 us
  Pallas kernels  78.8 us (99%)
    pallas_call x1, Pallas kernels, on_device(): pl.pallas_call(body, out_shape=(nodes, ends, ends), in_specs=[pl.BlockSpe...  77.2 us

profile of v3, /device:TPU:0, one launch (start us, length us, event | category | flops | bytes accessed | tf_op | source)
XLA Modules:
  0.0 79.4 jit_solution(5067055070650653722)
XLA Ops:
  0.6 77.2 %pfasst.1 = (f32[1,3,1,512,256]{4,3,2,1,0:T(8,128)S(1)}, f32[1,1,512,256]{3,2,1,0:T(8,128)S(1)}, f32[1,1,512,256]{3,2,1,0:T(8,128)S(1)}) custom-call(f32[1,1,512,256]{3,2,1,0:T(8,128)} %refs_0_.1, f32[1,3,1,512,256]{4,3,2,1,0:T(8,128)} %refs_1_.1, f32[1,512,256]{2,1,0:T(8,128)} %refs_2_.1), custom_call_target="tpu_custom_call" | custom-call | tf_op jit(solution)/shard_map/pfasst/pallas_call | solution.py:824
  77.9 1.6 %store.1 = (f32[1,3,1,512,256]{4,3,2,1,0:T(8,128)}, f32[1,1,512,256]{3,2,1,0:T(8,128)}, f32[1,1,512,256]{3,2,1,0:T(8,128)}) custom-call(f32[1,3,1,512,256]{4,3,2,1,0:T(8,128)S(1)} %get-tuple-element.6.fine, f32[1,1,512,256]{3,2,1,0:T(8,128)S(1)} %get-tuple-element.7.begin, f32[1,1,512,256]{3,2,1,0:T(8,128)S(1)} %get-tuple-element.8.coarse), custom_call_target="tpu_custom_call" | custom-call | tf_op jit(solution)/shard_map/store/pallas_call | solution.py:850

commit v4 on v3

--- a/solution.py
+++ b/solution.py
@@ -25,7 +25,8 @@
 ]
 MESH = pl.DeviceIdType.MESH
 PAD = 8
-SOUTH_PARTS = 2
+UNROLL = 16
+SHARES = (1, 1)
 
 KAPPA, NODE, START, RES, IMG, GAIN = 0, 1, 4, 5, 9, 13
 FIELDS = 15
@@ -69,7 +70,7 @@
     slices, slabs, ny, nz,
     start_in, nodes_in, kappa_in,
     fine_out, start_out, coarse_out,
-    field, lower, upper, faces, across, outgoing, result, mail, kept, marks, sums,
+    field, lower, upper, faces, across, outgoing, result, mail, kept, ahead, marks, sums,
     swap_s, swap_r, own_s, kin_s, kin_r, mail_s, mail_r, kept_s, kept_r, halo_s, halo_r, sum_s, sum_r, out_s, out_r, end_s, end_r, copy_s,
 ):
     f32 = jnp.float32
@@ -82,8 +83,9 @@
     win = half + PAD
     other = 1 - h
     partner = s + 1 - 2 * h
-    core = lax.rem(t, 2)
-    sibling = t + 1 - 2 * core
+    team = next(n for n in (4, 2, 1) if slices % n == 0)
+    rank = lax.rem(t, team)
+    early = lax.rem(t, 2) == 1
     first_row = pl.multiple_of(h * (half - PAD), 8)
     partner_row = pl.multiple_of(other * (half - PAD), 8)
     own = pl.multiple_of(PAD * h, 8)
@@ -119,6 +121,15 @@
             for space in (s, partner):
                 pl.semaphore_signal(barrier, inc=1, device_id=(tm, space), device_id_type=MESH)
 
+    far = [jnp.abs(rank - q) > 1 for q in range(team)]
+    for q in range(team):
+
+        @pl.when(far[q])
+        def _(q=q):
+            pl.semaphore_signal(
+                barrier, inc=1, device_id=(t - rank + q, s), device_id_type=MESH
+            )
+
     sources = [kappa_in.at[0]] + [nodes_in.at[0, j, 0] for j in range(3)] + [start_in.at[0, 0]]
     for k, source in enumerate(sources):
         pltpu.make_async_copy(
@@ -152,36 +163,25 @@
 
     pl.semaphore_wait(
         barrier,
-        slabs - 1 + 2 * has_next.astype(jnp.int32) + 2 * has_prev.astype(jnp.int32),
+        slabs - 1 + 2 * has_next.astype(jnp.int32) + 2 * has_prev.astype(jnp.int32)
+        + sum(f.astype(jnp.int32) for f in far),
     )
 
     tile = tile_of(win, 24)
     bounds = chunk_bounds(win, tile)
     chunks = len(bounds)
 
-    cuts = [8 * (win // 8 * q // 4) for q in range(5)]
-    parts = [(cuts[q], cuts[q + 1] - cuts[q]) for q in range(4)]
-    share = slices % 2 == 0
+    weights = [SHARES[q % 2] for q in range(team)]
+    cuts = [8 * (win // 8 * sum(weights[:q]) // sum(weights)) for q in range(team)] + [win]
+    parts = [(cuts[q], cuts[q + 1] - cuts[q]) for q in range(team)]
 
     def bounds_of(k, c):
         return bounds[c] if k else parts[c]
 
     def each_part(body):
-        for q in range(4):
-            if share:
-                pl.when(core == (q >= SOUTH_PARTS))(lambda q=q: body(q))
-            else:
-                body(q)
-
-    first = cuts[SOUTH_PARTS]
-    halves = [(0, first), (first, win - first)] if share else [(0, win)]
-
-    def each_half(body, mine_too=True):
-        for q, (lo, rows) in enumerate(halves):
-            if share and rows:
-                pl.when((core == q) == mine_too)(lambda lo=lo, rows=rows: body(lo, rows))
-            elif not share:
-                body(lo, rows)
+        for q in range(team):
+            if parts[q][1]:
+                pl.when(rank == q)(lambda q=q: body(q))
 
     def arrived(ref, sem):
         remote(ref, ref, sum_s.at[0], sem, t, partner).wait_recv()
@@ -208,21 +208,23 @@
             return field.at[KAPPA, other, pl.ds(PAD + lo, rows)]
         return (lower, upper)[e - 1].at[H_KAPPA, pl.ds(lo, rows)]
 
-    def kin_copy(e, lo, rows):
-        ref = kin_ref(e, lo, rows)
-        return remote(ref, ref, kin_s.at[e], kin_r.at[e], sibling, s)
-
-    def kin_start(e):
-        if share:
-            each_half(lambda lo, rows: kin_copy(e, lo, rows).start())
+    def kin_start(e, q):
+        ref = kin_ref(e, *parts[q])
+        for peer in range(team):
+            if peer != q:
+                remote(ref, ref, kin_s.at[e], kin_r.at[e], t - q + peer, s).start()
 
     def kin_wait(e):
-        if share:
-            each_half(lambda lo, rows: arrived(kin_ref(e, lo, rows), kin_r.at[e]), False)
+        for q in range(team):
+            rows = win - parts[q][1]
+            if rows:
+                pl.when(rank == q)(lambda rows=rows: arrived(kin_ref(e, 0, rows), kin_r.at[e]))
 
     def kin_sent(e):
-        if share:
-            each_half(lambda lo, rows: sent(kin_ref(e, lo, rows), kin_s.at[e]))
+        if team > 1:
+            each_part(
+                lambda q: sent(field.at[pl.ds(0, team - 1), 0, pl.ds(0, parts[q][1])], kin_s.at[e])
+            )
 
     pltpu.make_async_copy(outgoing, outgoing, own_s.at[1]).wait()
     each_part(lambda q: swap_start(0, q))
@@ -296,7 +298,8 @@
         def step(i, carry):
             return body(pl.multiple_of(offset + i * size, 8), carry)
 
-        return lax.fori_loop(0, rows // size, step, init)
+        count = rows // size
+        return lax.fori_loop(0, count, step, init, unroll=max(u for u in range(1, UNROLL + 1) if count % u == 0))
 
     def coefficients(b, carry):
         windows = [field[KAPPA, slab, pl.ds(b, tile + 2 * PAD), :] for slab in range(2)]
@@ -514,7 +517,7 @@
 
         loop(win, tile, body)
 
-    mailed = (GAIN, GAIN + 1, IMG + 1, IMG + 2)
+    mailed = (GAIN, GAIN + 1, IMG + 1, IMG + 2, RES + 3)
 
     def mail_copy(k):
         return remote(
@@ -526,20 +529,36 @@
         mail_copy(k).start()
         later(mail.at[k], mail_s.at[k])
 
-    def coarse_send(k, which=(0, 1)):
+    def coarse_send(k, which=(0, 1), cond=True):
         for slab, space in [((h, s), (other, partner))[w] for w in which]:
             copy = remote(
                 field.at[(RES + 3, IMG + 3)[k - 1], slab, pl.ds(PAD + own, half)],
                 kept.at[k, pl.ds(mine, half)], kept_s.at[k], kept_r.at[k], t + 1, space,
             )
-            pl.when(has_next)(copy.start)
+            pl.when(jnp.logical_and(has_next, cond))(copy.start)
 
     def kept_copy(k):
         if k == 0:
             src, dst = nodes_in.at[0, 2, 0], kept.at[0]
         else:
-            src, dst = marks.at[0], marks.at[1]
+            src, dst = marks.at[k - 3], marks.at[k - 1]
         return remote(src, dst, kept_s.at[k], kept_r.at[k], t + 1, s)
+
+    def marks_send(k, update):
+        for row in range(2):
+            marks[k - 3, row : row + 1, :] = jnp.broadcast_to(update[row], (1, 128))
+        pl.when(has_next)(kept_copy(k).start)
+
+    def marks_of(k):
+        arrived(marks.at[k - 1], kept_r.at[k])
+        return marks[k - 1, 0:1, 0:1], marks[k - 1, 1:2, 0:1]
+
+    def ahead_send(e):
+        copy = remote(
+            field.at[(RES + 2, IMG + 2)[e], h, pl.ds(PAD + own, half)], ahead.at[e],
+            kept_s.at[5], kept_r.at[5], t + 1, s,
+        )
+        pl.when(has_next)(copy.start)
 
     def finish(m, scalars, slab, ref, lo, rows):
         on_res, on_img = scalars
@@ -594,8 +613,7 @@
 
     def pass_kappa(q):
         swap_wait(0, q)
-        if share:
-            kin_copy(0, *parts[q]).start()
+        kin_start(0, q)
         first_hop(0, q, other)
 
     each_part(pass_kappa)
@@ -604,9 +622,9 @@
             swap_wait(k, c)
             first_hop(k, c, other)
         if c == 0:
-            each_half(lambda lo, rows: halo_wait(H_KAPPA, 0, lo, rows))
-            pl.when(has_lower)(lambda: kin_start(1))
-            pl.when(has_upper)(lambda: kin_start(2))
+            each_part(lambda q: halo_wait(H_KAPPA, 0, *parts[q]))
+            pl.when(has_lower)(lambda: each_part(lambda q: kin_start(1, q)))
+            pl.when(has_upper)(lambda: each_part(lambda q: kin_start(2, q)))
         if c == min(1, chunks - 1):
             kin_wait(0)
             pl.when(has_lower)(lambda: kin_wait(1))
@@ -661,7 +679,7 @@
         loop(rows, small, body, 0, lo)
 
     def finish_coarse():
-        on_res, on_img = marks[1, 0:1, 0:1], marks[1, 1:2, 0:1]
+        on_res, on_img = marks_of(3)
 
         def body(b, carry):
             at = pl.ds(b, small)
@@ -672,8 +690,6 @@
 
         loop(ny, small, body)
 
-    pl.when(has_next)(kept_copy(0).start)
-
     @pl.when(jnp.logical_not(has_prev))
     def _():
         pltpu.make_async_copy(start_in.at[0, 0], start_out.at[0, 0], copy_s.at[0]).start()
@@ -688,6 +704,7 @@
         halo_wait(H_GAIN + m, 0, 0, win)
 
     gain_send(0, range(0, 2))
+    pl.when(has_next)(kept_copy(0).start)
     halo_wait(H_RES, 0, 0, win)
     here = product(0)
     gain_send(0, range(2, 4))
@@ -696,7 +713,9 @@
     img_send(0, 1)
     gain_send(1, range(0, 2))
     coarse_residual()
-    coarse_send(1)
+    coarse_send(1, (0,))
+    pl.when(has_next)(mail_copy(4).start)
+    later(mail.at[4], mail_s.at[4], has_next)
     update = factors(0)
     gain_wait(0)
     img_wait(0, 1)
@@ -705,6 +724,14 @@
     mail_send(2)
     gain_send(1, range(2, 4))
     cross(1, here, local(1))
+
+    @pl.when(has_next)
+    def _():
+        mail_copy(4).wait_recv()
+        remote(
+            mail.at[4], kept.at[1, pl.ds(theirs, half)], kept_s.at[1], kept_r.at[1], t + 1, s
+        ).start()
+
     finish_start(update)
     gain_send(1, range(4, chunks))
     img_send(1, 1)
@@ -712,39 +739,47 @@
     coarse_halo()
     here_coarse = product(3)
     coarse_send(2, (0,))
+    coarse_send(2, (1,), early)
     update = factors(1)
     img_wait(1, 1)
     advance(1, update)
+    ahead_send(0)
     here = product(2)
+    ahead_send(1)
     mail_send(3)
     cross(3, here_coarse, local(3))
     cross(2, here, local(2))
-    coarse_send(2, (1,))
+    coarse_send(2, (1,), jnp.logical_not(early))
     finish_second(update)
 
+    def finish_next():
+        on_res, on_img = marks_of(4)
+        arrived(ahead, kept_r.at[5])
+
+        def body(b, carry):
+            at, rows = pl.ds(mine + b, small), pl.ds(b, small)
+            start_out[0, 0, at, :] = (
+                kept[0, at, :] + on_res * ahead[0, rows, :] - on_img * ahead[1, rows, :]
+            )
+            return carry
+
+        loop(half, small, body)
+
+    marks_send(3, factors(3))
+    mail_copy(3).wait_recv()
+    update = factors(2)
+    marks_send(4, update)
     pieces = 2 if half % (2 * small) == 0 else 1
     piece = half // pieces
-
-    def pass_on(at):
+    for c in range(pieces):
+        at = theirs + c * piece
+        finish_third(update, c * piece, piece)
         copy = remote(
             fine_out.at[0, 2, 0, pl.ds(at, piece)], start_out.at[0, 0, pl.ds(at, piece)],
             end_s.at[0], end_r.at[0], t + 1, s,
         )
         pl.when(has_next)(copy.start)
-
-    update = factors(3)
-    for row in range(2):
-        marks[0, row : row + 1, :] = jnp.broadcast_to(update[row], (1, 128))
-    pl.when(has_next)(kept_copy(3).start)
-
-    mail_copy(3).wait_recv()
-    update = factors(2)
-    for c in range(pieces):
-        finish(2, update, h, half_of(2, mine), c * piece, piece)
-        pass_on(mine + c * piece)
-    for c in range(pieces):
-        finish_third(update, c * piece, piece)
-        pass_on(theirs + c * piece)
+    finish(2, update, h, half_of(2, mine), 0, half)
 
     @pl.when(jnp.logical_not(has_prev))
     def _():
@@ -755,18 +790,19 @@
     def _():
         for k in range(3):
             arrived(kept.at[k], kept_r.at[k])
-        arrived(marks.at[1], kept_r.at[3])
         finish_coarse()
-        arrived(start_out.at[0, 0], end_r.at[0])
-
-    each_half(lambda lo, rows: sent(outgoing.at[0, pl.ds(lo, rows)], swap_s.at[0]))
+        finish_next()
+        arrived(start_out.at[0, 0, pl.ds(theirs, half)], end_r.at[0])
+
+    each_part(lambda q: sent(outgoing.at[0, pl.ds(*parts[q])], swap_s.at[0]))
     for side, cond in ((0, has_lower), (1, has_upper)):
 
         @pl.when(cond)
         def _(side=side):
-            each_half(
-                lambda lo, rows: sent(
-                    field.at[KAPPA, side, pl.ds(PAD + lo, rows)], halo_s.at[side, 0]
+            each_part(
+                lambda q: sent(
+                    field.at[KAPPA, side, pl.ds(PAD + parts[q][0], parts[q][1])],
+                    halo_s.at[side, 0],
                 )
             )
 
@@ -781,8 +817,10 @@
         halo_later(IMG + 2, 5, *pieces_of[0][side], 2, (side,))
     for k in range(3):
         later(kept.at[k], kept_s.at[k], has_next)
-    later(marks.at[0], kept_s.at[3], has_next)
-    later(fine_out.at[0, 2, 0], end_s.at[0], has_next)
+    for k in range(2):
+        later(marks.at[k], kept_s.at[3 + k], has_next)
+    later(ahead, kept_s.at[5], has_next)
+    later(fine_out.at[0, 2, 0, pl.ds(theirs, half)], end_s.at[0], has_next)
     later(sums.at[pl.ds(0, 4), pl.ds(0, slabs - 1)], sum_s.at[0])
     for ref, sem, cond in pending:
         if cond is None:
@@ -834,11 +872,12 @@
                 vmem(3, win, nz),
                 vmem(5, win, nz),
                 vmem(half, nz),
-                vmem(4, half, nz),
+                vmem(5, half, nz),
                 vmem(3, ny, nz),
-                vmem(2, 8, 128),
+                vmem(2, half, nz),
+                vmem(4, 8, 128),
                 vmem(4, slabs, 4, 128),
-                dma(2), dma(4 + 4 * chunks), dma(2), dma(3), dma(3), dma(4), dma(4), dma(4), dma(4),
+                dma(2), dma(4 + 4 * chunks), dma(2), dma(3), dma(3), dma(5), dma(5), dma(6), dma(6),
                 dma(2, 6), dma(2, 10 + chunks), dma(1), dma(4),
                 dma(1), dma(1), dma(1), dma(1), dma(2),
             ],

time: 79.6 us -> 76.3 us (0.959)
  Pallas kernels: 78.8 us -> 75.5 us
    pallas_call x1, Pallas kernels: 77.2 us -> 73.9 us  [on_device(): pl.pallas_call(body, out_shape=(nodes, ends, ends), in_specs=[pl.BlockSpe...]
where the time goes in v4:
time: 76.3 us; the launch traced here: 76.1 us
  Pallas kernels  75.5 us (99%)
    pallas_call x1, Pallas kernels, on_device(): pl.pallas_call(body, out_shape=(nodes, ends, ends), in_specs=[pl.BlockSpe...  73.9 us
    pallas_call x1, Pallas kernels, on_device(): pl.pallas_call(store, out_shape=tuple((jax.ShapeDtypeStruct(r.shape, jnp....  1.57 us

profile of v4, /device:TPU:0, one launch (start us, length us, event | category | flops | bytes accessed | tf_op | source)
XLA Modules:
  0.0 76.1 jit_solution(15434749004842511815)
XLA Ops:
  0.6 73.9 %pfasst.1 = (f32[1,3,1,512,256]{4,3,2,1,0:T(8,128)S(1)}, f32[1,1,512,256]{3,2,1,0:T(8,128)S(1)}, f32[1,1,512,256]{3,2,1,0:T(8,128)S(1)}) custom-call(f32[1,1,512,256]{3,2,1,0:T(8,128)} %refs_0_.1, f32[1,3,1,512,256]{4,3,2,1,0:T(8,128)} %refs_1_.1, f32[1,512,256]{2,1,0:T(8,128)} %refs_2_.1), custom_call_target="tpu_custom_call" | custom-call | tf_op jit(solution)/shard_map/pfasst/pallas_call | solution.py:862
  74.6 1.6 %store.1 = (f32[1,3,1,512,256]{4,3,2,1,0:T(8,128)}, f32[1,1,512,256]{3,2,1,0:T(8,128)}, f32[1,1,512,256]{3,2,1,0:T(8,128)}) custom-call(f32[1,3,1,512,256]{4,3,2,1,0:T(8,128)S(1)} %get-tuple-element.6.fine, f32[1,1,512,256]{3,2,1,0:T(8,128)S(1)} %get-tuple-element.7.begin, f32[1,1,512,256]{3,2,1,0:T(8,128)S(1)} %get-tuple-element.8.coarse), custom_call_target="tpu_custom_call" | custom-call | tf_op jit(solution)/shard_map/store/pallas_call | solution.py:889

commit v5 on v4

--- a/solution.py
+++ b/solution.py
@@ -49,7 +49,7 @@
 
 def chunk_bounds(rows, tile):
     tiles = rows // tile
-    parts = min(5, tiles)
+    parts = min(4, tiles)
     counts = [tiles // parts + (c < tiles % parts) for c in range(parts)]
     if counts[-1] > 1:
         counts[-1] -= 1
@@ -190,7 +190,7 @@
         remote(ref, ref, sem, sum_r.at[0], t, partner).wait_send()
 
     def swap_sem(k, c):
-        return swap_r.at[4 + (k - 1) * chunks + c if k else c]
+        return swap_r.at[1 + (k - 1) * chunks + c if k else 0]
 
     def swap_start(k, c):
         lo, rows = bounds_of(k, c)
@@ -396,14 +396,19 @@
         ((0, quarter), (quarter + PAD, quarter)),
     )
 
+    def rows_of(m, piece):
+        if m < 2:
+            return pieces_of[piece]
+        return (set_down, quarter), (set_up, quarter)
+
     def img_send(m, piece):
-        (lo_d, rows_d), (lo_u, rows_u) = pieces_of[piece]
+        (lo_d, rows_d), (lo_u, rows_u) = rows_of(m, piece)
         pl.when(has_lower)(down(IMG + m, H_IMG + m, piece, lo_d, rows_d).start)
         pl.when(has_upper)(up(IMG + m, H_IMG + m, piece, lo_u, rows_u).start)
 
     def img_wait(m, piece):
-        halo_wait(H_IMG + m, piece, *pieces_of[piece][0], (0,))
-        halo_wait(H_IMG + m, piece, *pieces_of[piece][1], (1,))
+        for side in range(2):
+            halo_wait(H_IMG + m, piece, *rows_of(m, piece)[side], (side,))
 
     nothing = jnp.zeros((8, nz), f32)
 
@@ -814,7 +819,7 @@
     halo_later(GAIN, 3, 0, win, 2)
     halo_later(IMG, 4, 0, win, 2)
     for side in range(2):
-        halo_later(IMG + 2, 5, *pieces_of[0][side], 2, (side,))
+        halo_later(IMG + 2, 5, *rows_of(2, 0)[side], 2, (side,))
     for k in range(3):
         later(kept.at[k], kept_s.at[k], has_next)
     for k in range(2):
@@ -877,7 +882,7 @@
                 vmem(2, half, nz),
                 vmem(4, 8, 128),
                 vmem(4, slabs, 4, 128),
-                dma(2), dma(4 + 4 * chunks), dma(2), dma(3), dma(3), dma(5), dma(5), dma(6), dma(6),
+                dma(2), dma(1 + 4 * chunks), dma(2), dma(3), dma(3), dma(5), dma(5), dma(6), dma(6),
                 dma(2, 6), dma(2, 10 + chunks), dma(1), dma(4),
                 dma(1), dma(1), dma(1), dma(1), dma(2),
             ],

time: 76.3 us -> 75.6 us (level)
  no operation moved by 1% of the time
where the time goes in v5:
time: 75.6 us; the launch traced here: 75.4 us
  Pallas kernels  74.8 us (99%)
    pallas_call x1, Pallas kernels, on_device(): pl.pallas_call(body, out_shape=(nodes, ends, ends), in_specs=[pl.BlockSpe...  73.2 us
    pallas_call x1, Pallas kernels, on_device(): pl.pallas_call(store, out_shape=tuple((jax.ShapeDtypeStruct(r.shape, jnp....  1.57 us

profile of v5, /device:TPU:0, one launch (start us, length us, event | category | flops | bytes accessed | tf_op | source)
XLA Modules:
  0.0 75.4 jit_solution(3609806424922249271)
XLA Ops:
  0.6 73.2 %pfasst.1 = (f32[1,3,1,512,256]{4,3,2,1,0:T(8,128)S(1)}, f32[1,1,512,256]{3,2,1,0:T(8,128)S(1)}, f32[1,1,512,256]{3,2,1,0:T(8,128)S(1)}) custom-call(f32[1,1,512,256]{3,2,1,0:T(8,128)} %refs_0_.1, f32[1,3,1,512,256]{4,3,2,1,0:T(8,128)} %refs_1_.1, f32[1,512,256]{2,1,0:T(8,128)} %refs_2_.1), custom_call_target="tpu_custom_call" | custom-call | tf_op jit(solution)/shard_map/pfasst/pallas_call | solution.py:867
  73.9 1.6 %store.1 = (f32[1,3,1,512,256]{4,3,2,1,0:T(8,128)}, f32[1,1,512,256]{3,2,1,0:T(8,128)}, f32[1,1,512,256]{3,2,1,0:T(8,128)}) custom-call(f32[1,3,1,512,256]{4,3,2,1,0:T(8,128)S(1)} %get-tuple-element.6.fine, f32[1,1,512,256]{3,2,1,0:T(8,128)S(1)} %get-tuple-element.7.begin, f32[1,1,512,256]{3,2,1,0:T(8,128)S(1)} %get-tuple-element.8.coarse), custom_call_target="tpu_custom_call" | custom-call | tf_op jit(solution)/shard_map/store/pallas_call | solution.py:894

commit v6 on v5

--- a/solution.py
+++ b/solution.py
@@ -241,12 +241,12 @@
         elif k < H_RES:
             slots = 1, 1 + c
         elif k == H_RES:
-            slots = 2, 1 + chunks
+            slots = 1, 1 + chunks
         elif k >= H_GAIN:
-            slots = 3, 2 + chunks + k - H_GAIN
+            slots = 1, 2 + chunks + k - H_GAIN
         else:
             m = k - H_IMG
-            slots = 4 + m // 2, 4 + chunks + (2 * m + c if m < 2 else 2 + m)
+            slots = 1 + m // 2, 4 + chunks + (2 * m + c if m < 2 else 2 + m)
         return halo_s.at[side, slots[0]], halo_r.at[side, slots[1]]
 
     def down(f, k, c, lo, rows):
@@ -527,12 +527,11 @@
     def mail_copy(k):
         return remote(
             field.at[mailed[k], other, pl.ds(PAD + own, half)], mail.at[k],
-            mail_s.at[k], mail_r.at[k], t, partner,
+            mail_s.at[k // 4], mail_r.at[k], t, partner,
         )
 
     def mail_send(k):
         mail_copy(k).start()
-        later(mail.at[k], mail_s.at[k])
 
     def coarse_send(k, which=(0, 1), cond=True):
         for slab, space in [((h, s), (other, partner))[w] for w in which]:
@@ -720,7 +719,8 @@
     coarse_residual()
     coarse_send(1, (0,))
     pl.when(has_next)(mail_copy(4).start)
-    later(mail.at[4], mail_s.at[4], has_next)
+    later(mail.at[4], mail_s.at[1], has_next)
+    later(mail.at[pl.ds(0, 4)], mail_s.at[0])
     update = factors(0)
     gain_wait(0)
     img_wait(0, 1)
@@ -814,12 +814,9 @@
     kin_sent(0)
     pl.when(has_lower)(lambda: kin_sent(1))
     pl.when(has_upper)(lambda: kin_sent(2))
-    halo_later(NODE, 1, 0, win, 3)
-    halo_later(RES, 2, 0, win)
-    halo_later(GAIN, 3, 0, win, 2)
-    halo_later(IMG, 4, 0, win, 2)
+    halo_later(0, 1, 0, win, 8)
     for side in range(2):
-        halo_later(IMG + 2, 5, *rows_of(2, 0)[side], 2, (side,))
+        halo_later(IMG + 2, 2, *rows_of(2, 0)[side], 2, (side,))
     for k in range(3):
         later(kept.at[k], kept_s.at[k], has_next)
     for k in range(2):
@@ -882,8 +879,8 @@
                 vmem(2, half, nz),
                 vmem(4, 8, 128),
                 vmem(4, slabs, 4, 128),
-                dma(2), dma(1 + 4 * chunks), dma(2), dma(3), dma(3), dma(5), dma(5), dma(6), dma(6),
-                dma(2, 6), dma(2, 10 + chunks), dma(1), dma(4),
+                dma(2), dma(1 + 4 * chunks), dma(2), dma(3), dma(3), dma(2), dma(5), dma(6), dma(6),
+                dma(2, 3), dma(2, 10 + chunks), dma(1), dma(4),
                 dma(1), dma(1), dma(1), dma(1), dma(2),
             ],
             compiler_params=pltpu.CompilerParams(

time: 75.6 us -> 75.5 us (level)
  no operation moved by 1% of the time
where the time goes in v6:
time: 75.5 us; the launch traced here: 75.4 us
  Pallas kernels  74.7 us (99%)
    pallas_call x1, Pallas kernels, on_device(): pl.pallas_call(body, out_shape=(nodes, ends, ends), in_specs=[pl.BlockSpe...  73.2 us
    pallas_call x1, Pallas kernels, on_device(): pl.pallas_call(store, out_shape=tuple((jax.ShapeDtypeStruct(r.shape, jnp....  1.57 us

profile of v6, /device:TPU:0, one launch (start us, length us, event | category | flops | bytes accessed | tf_op | source)
XLA Modules:
  0.0 75.4 jit_solution(2883079996386283198)
XLA Ops:
  0.6 73.2 %pfasst.1 = (f32[1,3,1,512,256]{4,3,2,1,0:T(8,128)S(1)}, f32[1,1,512,256]{3,2,1,0:T(8,128)S(1)}, f32[1,1,512,256]{3,2,1,0:T(8,128)S(1)}) custom-call(f32[1,1,512,256]{3,2,1,0:T(8,128)} %refs_0_.1, f32[1,3,1,512,256]{4,3,2,1,0:T(8,128)} %refs_1_.1, f32[1,512,256]{2,1,0:T(8,128)} %refs_2_.1), custom_call_target="tpu_custom_call" | custom-call | tf_op jit(solution)/shard_map/pfasst/pallas_call | solution.py:864
  73.8 1.6 %store.1 = (f32[1,3,1,512,256]{4,3,2,1,0:T(8,128)}, f32[1,1,512,256]{3,2,1,0:T(8,128)}, f32[1,1,512,256]{3,2,1,0:T(8,128)}) custom-call(f32[1,3,1,512,256]{4,3,2,1,0:T(8,128)S(1)} %get-tuple-element.6.fine, f32[1,1,512,256]{3,2,1,0:T(8,128)S(1)} %get-tuple-element.7.begin, f32[1,1,512,256]{3,2,1,0:T(8,128)S(1)} %get-tuple-element.8.coarse), custom_call_target="tpu_custom_call" | custom-call | tf_op jit(solution)/shard_map/store/pallas_call | solution.py:891
